TPU v7x, 32 devices: a whole 2x2x4 slice. The times are simulated.
32 devices in a mesh: gx: 4 (over y, x), gy: 4 (over z), gz: 2 (over core).
Axes of the slice: x: 2, y: 2, z: 4, core: 2. Of those that a mesh axis runs over, the one named last changes fastest.
Arguments:
- s_blocks: bfloat16 [32, 4, 128, 128], P(('gx', 'gy', 'gz')), may hold values from -1 to 2
- s_columns: int32 [32, 4], P(('gx', 'gy', 'gz')), may hold values from 0 to 6, as said below
- new_home: int32 [32], P(('gx', 'gy', 'gz')), may hold values from 0 to 1, as said below
- z_pattern: int32 [32, 7], P(('gx', 'gy', 'gz')), may hold values 0 or 1
- y_pattern: int32 [32, 7], P(('gx', 'gy', 'gz')), may hold values 0 or 1
Outputs:
- z_out: bfloat16 [32, 128, 7, 128], P(('gx', 'gy', 'gz'))
- y_out: bfloat16 [32, 128, 7, 128], P(('gx', 'gy', 'gz'))
Inputs may be any that keep to these rules, and one draw needn't show every extreme that they name: new_home = 1 * (new gz index) + new slot; among the clusters of devices that share gx and gy indices each value occurs once, and the 1 clusters of one device go to 1 different devices. `s_columns`: the entries of a row are distinct, and the first is the cluster's own diagonal block in the new layout (part 0, its new slot).
All inputs are finite; a program needn't handle non-finite values. No bound on the sum of `z_pattern` or of `y_pattern` on one device may be relied on, other than what follows from the above.
Results may differ from a plain program's by a relative error of at most 0.0058.
Values may be sent and summed in bfloat16 or wider, within the bound.
No kernel may reach another device: no remote copies, remote signals or barrier semaphores. Data moves between devices by JAX's collectives and lax.ppermute only.
A program may use at most 64 MiB of HBM per device.

v0:
```python
import jax
import jax.numpy as jnp
from jax import lax
from jax.sharding import PartitionSpec as P


def from_behind(x, axis, by):
    count = lax.axis_size(axis)
    pairs = [(i, i + by) for i in range(count) if 0 <= i + by < count]
    return lax.ppermute(x, axis, pairs)


def expand(retain, matrix):
    slot_count = retain.shape[0]
    block_size = matrix.shape[0] // slot_count
    blocked = matrix.reshape(slot_count, block_size, 7, slot_count, block_size)
    chosen = jnp.where(retain[:, None, :, :, None], blocked, jnp.zeros((), matrix.dtype))
    return chosen.reshape(matrix.shape)


def block_product(left, right, halo):
    rows_total = left.shape[0]
    stacked = jnp.concatenate([right[:, 0, :][None], halo[:, :, 1, :]], axis=0).reshape(
        7 * rows_total, rows_total
    )
    own_column = jnp.dot(
        left.reshape(rows_total, 7 * rows_total), stacked, preferred_element_type=jnp.float32
    )
    across = jnp.dot(
        left[:, 0, :],
        right[:, 1:, :].reshape(rows_total, 6 * rows_total),
        preferred_element_type=jnp.float32,
    ).reshape(rows_total, 6, rows_total)
    across = across + jnp.einsum(
        "irj,rjk->irk", left[:, 1:, :], halo[:, :, 0, :], preferred_element_type=jnp.float32
    )
    return jnp.concatenate([own_column[:, None, :], across], axis=1)


def gather_halo(matrices):

    def packed(facing):
        return jnp.stack(
            [matrix[:, which_block, :] for matrix in matrices for which_block in (0, facing)],
            axis=1,
        )

    arrived = {}
    for offset in (1, -1):
        arrived["x", offset] = from_behind(packed(2 if offset == 1 else 1), "gx", offset)
    for offset in (1, -1):
        arrived["y", offset] = from_behind(packed(4 if offset == 1 else 3), "gy", offset)
    for offset in (1, -1):
        arrived["z", offset] = from_behind(packed(6 if offset == 1 else 5), "gz", offset)
    ordered = [
        arrived["x", 1],
        arrived["x", -1],
        arrived["y", 1],
        arrived["y", -1],
        arrived["z", 1],
        arrived["z", -1],
    ]
    return jnp.stack(ordered, axis=0)


def body(s_blocks, s_columns, new_home, z_pattern, y_pattern):
    slot_count = s_blocks.shape[0]
    block_count = s_blocks.shape[1]
    block_size = s_blocks.shape[2]
    rows_total = slot_count * block_size
    lanes = lax.axis_size("gz")
    targets = jnp.arange(lanes, dtype=jnp.int32)
    dest_device = new_home // slot_count
    dest_slot = new_home % slot_count
    chosen = dest_device[None, :] == targets[:, None]
    outgoing = jnp.einsum(
        "tj,jkab->tkab", chosen.astype(jnp.bfloat16), s_blocks, preferred_element_type=jnp.float32
    ).astype(jnp.bfloat16)
    labels = jnp.concatenate(
        [s_columns, dest_slot[:, None], jnp.ones((slot_count, 1), jnp.int32)], axis=1
    )
    label_out = jnp.sum(jnp.where(chosen[:, :, None], labels[None], 0), axis=1)
    arrived_blocks, arrived_labels = (
        lax.all_to_all(outgoing, "gz", split_axis=0, concat_axis=0, tiled=True),
        lax.all_to_all(label_out, "gz", split_axis=0, concat_axis=0, tiled=True),
    )
    present = arrived_labels[:, block_count + 1] == 1
    landing = arrived_labels[:, block_count]
    column_of = arrived_labels[:, :block_count]
    column_ids = jnp.arange(7 * slot_count, dtype=jnp.int32)
    slot_ids = jnp.arange(slot_count, dtype=jnp.int32)
    routing = (
        present[None, None, :, None]
        & (landing[None, None, :, None] == slot_ids[:, None, None, None])
        & (column_of[None, None, :, :] == column_ids[None, :, None, None])
    )
    dense = jnp.einsum(
        "qcsk,skab->qacb",
        routing.astype(jnp.bfloat16),
        arrived_blocks,
        preferred_element_type=jnp.float32,
    ).astype(jnp.bfloat16)
    start = dense.reshape(rows_total, 7, rows_total)
    place_x = lax.axis_index("gx")
    place_y = lax.axis_index("gy")
    place_z = lax.axis_index("gz")
    valid = jnp.stack(
        [
            place_x >= 0,
            place_x > 0,
            place_x < lax.axis_size("gx") - 1,
            place_y > 0,
            place_y < lax.axis_size("gy") - 1,
            place_z > 0,
            place_z < lanes - 1,
        ]
    )
    diagonal = (jnp.arange(7)[None, :, None] == 0) & (
        slot_ids[:, None, None] == slot_ids[None, None, :]
    )
    retain_valid = valid[None, :, None]
    retain_y = ((y_pattern.reshape(slot_count, 7, slot_count) == 1) | diagonal) & valid[
        None, :, None
    ]
    retain_z = ((z_pattern.reshape(slot_count, 7, slot_count) == 1) | diagonal) & valid[
        None, :, None
    ]
    identity = jnp.concatenate(
        [
            jnp.eye(rows_total, dtype=jnp.float32)[:, None, :],
            jnp.zeros((rows_total, 6, rows_total), jnp.float32),
        ],
        axis=1,
    )
    square = expand(retain_valid, start)
    middle = expand(retain_y, 1.5 * identity - 0.5 * square.astype(jnp.float32)).astype(
        jnp.bfloat16
    )
    halo_middle = gather_halo([middle])
    square_next = expand(retain_y, block_product(square, middle, halo_middle)).astype(jnp.bfloat16)
    inverse = expand(retain_z, middle)
    square = square_next
    both_halos = gather_halo([square, inverse])
    halo_square = both_halos[:, :, 0:2, :]
    halo_inverse = both_halos[:, :, 2:4, :]
    quad = expand(retain_y, block_product(inverse, square, halo_square))
    middle = expand(retain_y, 1.5 * identity - 0.5 * quad).astype(jnp.bfloat16)
    halo_middle = gather_halo([middle])
    square_next = expand(retain_y, block_product(square, middle, halo_middle)).astype(jnp.bfloat16)
    inverse = expand(retain_z, block_product(middle, inverse, halo_inverse)).astype(jnp.bfloat16)
    out_shape = (slot_count, block_size, 7 * slot_count, block_size)
    return (inverse.reshape(out_shape), square_next.reshape(out_shape))


def solution(mesh):
    in_specs = (
        P(("gx", "gy", "gz"), None, None, None),
        P(("gx", "gy", "gz"), None),
        P(("gx", "gy", "gz")),
        P(("gx", "gy", "gz"), None),
        P(("gx", "gy", "gz"), None),
    )
    out_specs = (P(("gx", "gy", "gz"), None, None, None), P(("gx", "gy", "gz"), None, None, None))
    return jax.shard_map(body, mesh=mesh, in_specs=in_specs, out_specs=out_specs, check_vma=False)
```

profile of v0, /device:TPU:13, one launch (start us, length us, event | category | flops | bytes accessed | tf_op | source)
XLA Modules:
  0.0 84.2 jit_solution(144621326459198887)
XLA Ops:
  1.3 0.6 copy-done.6
  2.0 0.6 broadcast_select_fusion.1
  2.6 3.9 %all-to-all-start.1 = ((s32[2,1,6]{2,1,0:T(1,128)}), s32[2,1,6]{2,1,0:T(1,128)S(1)}, u32[]{:S(2)}, u32[]{:S(2)}) async-start(s32[2,1,6]{2,1,0:T(1,128)} %broadcast_select_fusion.1), calls=%async_computation.1 | async-start | bytes 2048 | tf_op jit(solution)/shard_map/all_to_all | solution.py:85
  6.6 0.9 %bitcast_convert_fusion = f32[4,128,128]{2,1,0:T(8,128)S(1)} fusion(bf16[1,4,128,128]{3,2,1,0:T(8,128)(2,1)} %param.5), kind=kLoop, calls=%fused_computation.82 | loop fusion | flops 65536 | bytes 393216 | tf_op jit(solution)/shard_map/convert.7
  7.7 0.9 %multiply_convert_fusion = bf16[2,4,128,128]{3,1,2,0:T(4,128)(2,1)} fusion(f32[4,128,128]{2,0,1:T(4,128)S(1)} %copy.145, f32[2]{0:T(128)S(1)} %fusion.65), kind=kLoop, calls=%fused_computation.22 | loop fusion | flops 262144 | bytes 524296 | tf_op jit(solution)/shard_map/convert_element_type | solution.py:78
  8.6 3.5 %all-to-all-start = ((bf16[2,4,128,128]{3,1,2,0:T(4,128)(2,1)}), bf16[2,4,128,128]{3,1,2,0:T(4,128)(2,1)S(1)}, u32[]{:S(2)}, u32[]{:S(2)}) async-start(bf16[2,4,128,128]{3,1,2,0:T(4,128)(2,1)} %multiply_convert_fusion), calls=%async_computation | async-start | bytes 524288 | tf_op jit(solution)/shard_map/all_to_all | solution.py:84
  12.4 0.5 copy-done.4
  12.9 0.3 all-to-all-done
  13.2 0.5 broadcast_select_fusion
  13.7 0.3 fusion.76
  14.0 0.5 pad_maximum_fusion.16
  14.6 3.1 %collective-permute-start = (bf16[128,2,128]{2,1,0:T(2,128)(2,1)S(1)}, bf16[128,2,128]{2,1,0:T(2,128)(2,1)S(1)}, u32[]{:S(2)}, u32[]{:S(2)}) collective-permute-start(bf16[128,2,128]{2,1,0:T(2,128)(2,1)S(1)} %get-tuple-element.50), channel_id=1, source_target_pairs={{0,8},{8,16},{16,24},{1,9},{9,17},{17,25},{2,10},{10,18},{18,26},{... | collective-permute-start | bytes 196616 | tf_op jit(solution)/shard_map/ppermute | solution.py:10
  17.8 3.1 %collective-permute-start.1 = (bf16[128,2,128]{2,1,0:T(2,128)(2,1)S(1)}, bf16[128,2,128]{2,1,0:T(2,128)(2,1)S(1)}, u32[]{:S(2)}, u32[]{:S(2)}) collective-permute-start(bf16[128,2,128]{2,1,0:T(2,128)(2,1)S(1)} %stack.189), channel_id=1, source_target_pairs={{8,0},{16,8},{24,16},{9,1},{17,9},{25,17},{10,2},{18,10},{26,18},{... | collective-permute-start | bytes 196616 | tf_op jit(solution)/shard_map/ppermute | solution.py:10
  20.8 3.2 %collective-permute-start.2 = (bf16[128,2,128]{2,1,0:T(2,128)(2,1)S(1)}, bf16[128,2,128]{2,1,0:T(2,128)(2,1)S(1)}, u32[]{:S(2)}, u32[]{:S(2)}) collective-permute-start(bf16[128,2,128]{2,1,0:T(2,128)(2,1)S(1)} %get-tuple-element.47), channel_id=1, source_target_pairs={{0,2},{2,4},{4,6},{1,3},{3,5},{5,7},{8,10},{10,12},{12,14},{9,11},... | collective-permute-start | bytes 196616 | tf_op jit(solution)/shard_map/ppermute | solution.py:10
  24.0 2.1 %collective-permute-start.3 = (bf16[128,2,128]{2,1,0:T(2,128)(2,1)S(1)}, bf16[128,2,128]{2,1,0:T(2,128)(2,1)S(1)}, u32[]{:S(2)}, u32[]{:S(2)}) collective-permute-start(bf16[128,2,128]{2,1,0:T(2,128)(2,1)S(1)} %get-tuple-element.48), channel_id=1, source_target_pairs={{2,0},{4,2},{6,4},{3,1},{5,3},{7,5},{10,8},{12,10},{14,12},{11,9},... | collective-permute-start | bytes 196616 | tf_op jit(solution)/shard_map/ppermute | solution.py:10
  26.1 1.3 %collective-permute-start.4 = (bf16[128,2,128]{2,1,0:T(2,128)(2,1)S(1)}, bf16[128,2,128]{2,1,0:T(2,128)(2,1)S(1)}, u32[]{:S(2)}, u32[]{:S(2)}) collective-permute-start(bf16[128,2,128]{2,1,0:T(2,128)(2,1)S(1)} %get-tuple-element.49), channel_id=1, source_target_pairs={{0,1},{2,3},{4,5},{6,7},{8,9},{10,11},{12,13},{14,15},{16,17},{18,... | collective-permute-start | bytes 196616 | tf_op jit(solution)/shard_map/ppermute | solution.py:10
  27.5 0.2 copy.149
  27.8 0.3 fusion.75
  28.6 0.2 copy.147
  28.8 0.2 copy.153
  29.3 0.6 copy.255
  29.9 3.4 %collective-permute-start.5 = (bf16[128,2,128]{2,1,0:T(2,128)(2,1)S(1)}, bf16[128,2,128]{2,1,0:T(2,128)(2,1)S(1)}, u32[]{:S(2)}, u32[]{:S(2)}) collective-permute-start(bf16[128,2,128]{2,1,0:T(2,128)(2,1)S(1)} %get-tuple-element.46), channel_id=1, source_target_pairs={{1,0},{3,2},{5,4},{7,6},{9,8},{11,10},{13,12},{15,14},{17,16},{19,... | collective-permute-start | bytes 196616 | tf_op jit(solution)/shard_map/ppermute | solution.py:10
  33.6 0.5 collective-permute-done.5
  34.2 0.6 fusion.72
  34.9 0.3 fusion.41
  35.2 0.2 copy.152
  35.5 0.3 fusion.77
  36.0 0.3 fusion.74
  36.3 0.4 copy-done
  36.9 0.9 %fusion.49 = (bf16[128,4,128]{2,1,0:T(4,128)(2,1)S(1)}, bf16[128,4,128]{2,1,0:T(4,128)(2,1)S(1)}, bf16[128,4,128]{2,1,0:T(4,128)(2,1)S(1)}, bf16[128,4,128]{2,1,0:T(4,128)(2,1)S(1)}) fusion(bf16[128,1,128]{2,1,0:T(2,128)(2,1)S(1)} %get-tuple-element.30, bf16[128,1,128]{2,1,0:T(2,128)(2,1)S(1)} %get-tuple-element.24, ...), kind=kLoop, calls=%fused_computation.80 | loop fusion | flops 1703936 | bytes 851968 | tf_op jit(solution)/shard_map/stack | solution.py:43
  37.8 3.2 %collective-permute-start.8 = (bf16[128,4,128]{2,1,0:T(4,128)(2,1)S(1)}, bf16[128,4,128]{2,1,0:T(4,128)(2,1)S(1)}, u32[]{:S(2)}, u32[]{:S(2)}) collective-permute-start(bf16[128,4,128]{2,1,0:T(4,128)(2,1)S(1)} %get-tuple-element.38), channel_id=1, source_target_pairs={{0,2},{2,4},{4,6},{1,3},{3,5},{5,7},{8,10},{10,12},{12,14},{9,11},... | collective-permute-start | bytes 393224 | tf_op jit(solution)/shard_map/ppermute | solution.py:10
  41.0 0.3 fusion.45
  41.3 2.2 %collective-permute-start.6 = (bf16[128,4,128]{2,1,0:T(4,128)(2,1)S(1)}, bf16[128,4,128]{2,1,0:T(4,128)(2,1)S(1)}, u32[]{:S(2)}, u32[]{:S(2)}) collective-permute-start(bf16[128,4,128]{2,1,0:T(4,128)(2,1)S(1)} %fusion.45), channel_id=1, source_target_pairs={{0,8},{8,16},{16,24},{1,9},{9,17},{17,25},{2,10},{10,18},{18,26},{... | collective-permute-start | bytes 393224 | tf_op jit(solution)/shard_map/ppermute | solution.py:10
  43.7 4.0 %collective-permute-start.7 = (bf16[128,4,128]{2,1,0:T(4,128)(2,1)S(1)}, bf16[128,4,128]{2,1,0:T(4,128)(2,1)S(1)}, u32[]{:S(2)}, u32[]{:S(2)}) collective-permute-start(bf16[128,4,128]{2,1,0:T(4,128)(2,1)S(1)} %pad_maximum_fusion.11), channel_id=1, source_target_pairs={{8,0},{16,8},{24,16},{9,1},{17,9},{25,17},{10,2},{18,10},{26,18},{... | collective-permute-start | bytes 393224 | tf_op jit(solution)/shard_map/ppermute | solution.py:10
  47.7 2.1 %collective-permute-start.9 = (bf16[128,4,128]{2,1,0:T(4,128)(2,1)S(1)}, bf16[128,4,128]{2,1,0:T(4,128)(2,1)S(1)}, u32[]{:S(2)}, u32[]{:S(2)}) collective-permute-start(bf16[128,4,128]{2,1,0:T(4,128)(2,1)S(1)} %get-tuple-element.39), channel_id=1, source_target_pairs={{2,0},{4,2},{6,4},{3,1},{5,3},{7,5},{10,8},{12,10},{14,12},{11,9},... | collective-permute-start | bytes 393224 | tf_op jit(solution)/shard_map/ppermute | solution.py:10
  49.8 1.3 %collective-permute-start.10 = (bf16[128,4,128]{2,1,0:T(4,128)(2,1)S(1)}, bf16[128,4,128]{2,1,0:T(4,128)(2,1)S(1)}, u32[]{:S(2)}, u32[]{:S(2)}) collective-permute-start(bf16[128,4,128]{2,1,0:T(4,128)(2,1)S(1)} %get-tuple-element.40), channel_id=1, source_target_pairs={{0,1},{2,3},{4,5},{6,7},{8,9},{10,11},{12,13},{14,15},{16,17},{18,... | collective-permute-start | bytes 393224 | tf_op jit(solution)/shard_map/ppermute | solution.py:10
  51.5 0.2 copy.162
  51.7 3.6 %collective-permute-start.11 = (bf16[128,4,128]{2,1,0:T(4,128)(2,1)S(1)}, bf16[128,4,128]{2,1,0:T(4,128)(2,1)S(1)}, u32[]{:S(2)}, u32[]{:S(2)}) collective-permute-start(bf16[128,4,128]{2,1,0:T(4,128)(2,1)S(1)} %get-tuple-element.37), channel_id=1, source_target_pairs={{1,0},{3,2},{5,4},{7,6},{9,8},{11,10},{13,12},{15,14},{17,16},{19,... | collective-permute-start | bytes 393224 | tf_op jit(solution)/shard_map/ppermute | solution.py:10
  55.7 0.4 collective-permute-done.11
  56.2 1.6 %fusion.70 = (bf16[6,128,1,128]{3,2,1,0:T(2,128)(2,1)S(1)}, bf16[6,128,1,128]{3,2,1,0:T(2,128)(2,1)S(1)}, bf16[6,128,1,128]{3,2,1,0:T(2,128)(2,1)S(1)}, bf16[6,128,1,128]{3,2,1,0:T(2,128)(2,1)S(1)}) fusion(bf16[6,128,4,128]{3,2,1,0:T(4,128)(2,1)S(1)} %bitcast_dynamic-update-slice_fusion), kind=kLoop, calls=%fused_computation.141 | loop fusion | bytes 1572864 | tf_op jit(solution)/shard_map/slice | solution.py:23
  57.7 0.9 %copy.186 = bf16[6,128,1,128]{1,3,0,2:T(8,128)(2,1)} copy(bf16[6,128,1,128]{3,2,1,0:T(2,128)(2,1)S(1)} %get-tuple-element.8) | data formatting | bytes 393216 | tf_op jit(solution)/shard_map/squeeze | solution.py:23
  58.7 0.3 fusion.38
  59.0 0.2 copy.161
  59.2 0.7 copy-done.2
  59.9 0.2 fusion.13
  60.2 0.3 fusion.8
  60.5 0.3 fusion.73
  61.1 0.5 pad_maximum_fusion.21
  61.6 1.9 %collective-permute-start.12 = (bf16[128,2,128]{2,1,0:T(2,128)(2,1)S(1)}, bf16[128,2,128]{2,1,0:T(2,128)(2,1)S(1)}, u32[]{:S(2)}, u32[]{:S(2)}) collective-permute-start(bf16[128,2,128]{2,1,0:T(2,128)(2,1)S(1)} %get-tuple-element.45), channel_id=1, source_target_pairs={{0,8},{8,16},{16,24},{1,9},{9,17},{17,25},{2,10},{10,18},{18,26},{... | collective-permute-start | bytes 196616 | tf_op jit(solution)/shard_map/ppermute | solution.py:10
  64.0 0.7 copy-done.3
  64.7 0.2 convolution_bitcast_fusion.4
  64.9 0.3 fusion.4
  65.2 0.8 fusion.11
  66.1 4.3 %collective-permute-start.13 = (bf16[128,2,128]{2,1,0:T(2,128)(2,1)S(1)}, bf16[128,2,128]{2,1,0:T(2,128)(2,1)S(1)}, u32[]{:S(2)}, u32[]{:S(2)}) collective-permute-start(bf16[128,2,128]{2,1,0:T(2,128)(2,1)S(1)} %stack.190), channel_id=1, source_target_pairs={{8,0},{16,8},{24,16},{9,1},{17,9},{25,17},{10,2},{18,10},{26,18},{... | collective-permute-start | bytes 196616 | tf_op jit(solution)/shard_map/ppermute | solution.py:10
  70.3 3.2 %collective-permute-start.14 = (bf16[128,2,128]{2,1,0:T(2,128)(2,1)S(1)}, bf16[128,2,128]{2,1,0:T(2,128)(2,1)S(1)}, u32[]{:S(2)}, u32[]{:S(2)}) collective-permute-start(bf16[128,2,128]{2,1,0:T(2,128)(2,1)S(1)} %get-tuple-element.42), channel_id=1, source_target_pairs={{0,2},{2,4},{4,6},{1,3},{3,5},{5,7},{8,10},{10,12},{12,14},{9,11},... | collective-permute-start | bytes 196616 | tf_op jit(solution)/shard_map/ppermute | solution.py:10
  73.5 2.1 %collective-permute-start.15 = (bf16[128,2,128]{2,1,0:T(2,128)(2,1)S(1)}, bf16[128,2,128]{2,1,0:T(2,128)(2,1)S(1)}, u32[]{:S(2)}, u32[]{:S(2)}) collective-permute-start(bf16[128,2,128]{2,1,0:T(2,128)(2,1)S(1)} %get-tuple-element.43), channel_id=1, source_target_pairs={{2,0},{4,2},{6,4},{3,1},{5,3},{7,5},{10,8},{12,10},{14,12},{11,9},... | collective-permute-start | bytes 196616 | tf_op jit(solution)/shard_map/ppermute | solution.py:10
  75.6 1.3 %collective-permute-start.16 = (bf16[128,2,128]{2,1,0:T(2,128)(2,1)S(1)}, bf16[128,2,128]{2,1,0:T(2,128)(2,1)S(1)}, u32[]{:S(2)}, u32[]{:S(2)}) collective-permute-start(bf16[128,2,128]{2,1,0:T(2,128)(2,1)S(1)} %get-tuple-element.44), channel_id=1, source_target_pairs={{0,1},{2,3},{4,5},{6,7},{8,9},{10,11},{12,13},{14,15},{16,17},{18,... | collective-permute-start | bytes 196616 | tf_op jit(solution)/shard_map/ppermute | solution.py:10
  77.0 3.4 %collective-permute-start.17 = (bf16[128,2,128]{2,1,0:T(2,128)(2,1)S(1)}, bf16[128,2,128]{2,1,0:T(2,128)(2,1)S(1)}, u32[]{:S(2)}, u32[]{:S(2)}) collective-permute-start(bf16[128,2,128]{2,1,0:T(2,128)(2,1)S(1)} %get-tuple-element.41), channel_id=1, source_target_pairs={{1,0},{3,2},{5,4},{7,6},{9,8},{11,10},{13,12},{15,14},{17,16},{19,... | collective-permute-start | bytes 196616 | tf_op jit(solution)/shard_map/ppermute | solution.py:10
  80.7 0.5 collective-permute-done.17
  81.3 0.6 fusion.71
  82.0 0.9 %copy-done.1 = bf16[128,7,128]{2,1,0:T(8,128)(2,1)S(1)} copy-done((bf16[128,7,128]{2,1,0:T(8,128)(2,1)S(1)}, bf16[128,7,128]{2,1,0:T(8,128)(2,1)}, u32[]{:S(2)}) %copy-start.1) | copy-done | bytes 229400
  82.9 0.2 convolution_bitcast_fusion.3
  83.1 0.3 fusion.2
  83.4 0.8 fusion.12
  (80 shorter events, 4.5 us)
Async XLA Ops:
  1.3 0.7 copy-start.6
  2.6 5.9 %all-to-all-start.1 = ((s32[2,1,6]{2,1,0:T(1,128)}), s32[2,1,6]{2,1,0:T(1,128)S(1)}, u32[]{:S(2)}, u32[]{:S(2)}) async-start(s32[2,1,6]{2,1,0:T(1,128)} %broadcast_select_fusion.1), calls=%async_computation.1 | async-start | bytes 2048 | tf_op jit(solution)/shard_map/all_to_all | solution.py:85
  8.6 4.7 %all-to-all-start = ((bf16[2,4,128,128]{3,1,2,0:T(4,128)(2,1)}), bf16[2,4,128,128]{3,1,2,0:T(4,128)(2,1)S(1)}, u32[]{:S(2)}, u32[]{:S(2)}) async-start(bf16[2,4,128,128]{3,1,2,0:T(4,128)(2,1)} %multiply_convert_fusion), calls=%async_computation | async-start | bytes 524288 | tf_op jit(solution)/shard_map/all_to_all | solution.py:84
  12.2 0.7 copy-start.4
  12.2 0.7 copy-start.5
  14.6 15.3 %collective-permute-start = (bf16[128,2,128]{2,1,0:T(2,128)(2,1)S(1)}, bf16[128,2,128]{2,1,0:T(2,128)(2,1)S(1)}, u32[]{:S(2)}, u32[]{:S(2)}) collective-permute-start(bf16[128,2,128]{2,1,0:T(2,128)(2,1)S(1)} %get-tuple-element.50), channel_id=1, source_target_pairs={{0,8},{8,16},{16,24},{1,9},{9,17},{17,25},{2,10},{10,18},{18,26},{... | collective-permute-start | bytes 196616 | tf_op jit(solution)/shard_map/ppermute | solution.py:10
  17.8 15.6 %collective-permute-start.1 = (bf16[128,2,128]{2,1,0:T(2,128)(2,1)S(1)}, bf16[128,2,128]{2,1,0:T(2,128)(2,1)S(1)}, u32[]{:S(2)}, u32[]{:S(2)}) collective-permute-start(bf16[128,2,128]{2,1,0:T(2,128)(2,1)S(1)} %stack.189), channel_id=1, source_target_pairs={{8,0},{16,8},{24,16},{9,1},{17,9},{25,17},{10,2},{18,10},{26,18},{... | collective-permute-start | bytes 196616 | tf_op jit(solution)/shard_map/ppermute | solution.py:10
  20.8 12.6 %collective-permute-start.2 = (bf16[128,2,128]{2,1,0:T(2,128)(2,1)S(1)}, bf16[128,2,128]{2,1,0:T(2,128)(2,1)S(1)}, u32[]{:S(2)}, u32[]{:S(2)}) collective-permute-start(bf16[128,2,128]{2,1,0:T(2,128)(2,1)S(1)} %get-tuple-element.47), channel_id=1, source_target_pairs={{0,2},{2,4},{4,6},{1,3},{3,5},{5,7},{8,10},{10,12},{12,14},{9,11},... | collective-permute-start | bytes 196616 | tf_op jit(solution)/shard_map/ppermute | solution.py:10
  24.0 9.5 %collective-permute-start.3 = (bf16[128,2,128]{2,1,0:T(2,128)(2,1)S(1)}, bf16[128,2,128]{2,1,0:T(2,128)(2,1)S(1)}, u32[]{:S(2)}, u32[]{:S(2)}) collective-permute-start(bf16[128,2,128]{2,1,0:T(2,128)(2,1)S(1)} %get-tuple-element.48), channel_id=1, source_target_pairs={{2,0},{4,2},{6,4},{3,1},{5,3},{7,5},{10,8},{12,10},{14,12},{11,9},... | collective-permute-start | bytes 196616 | tf_op jit(solution)/shard_map/ppermute | solution.py:10
  26.1 7.5 %collective-permute-start.4 = (bf16[128,2,128]{2,1,0:T(2,128)(2,1)S(1)}, bf16[128,2,128]{2,1,0:T(2,128)(2,1)S(1)}, u32[]{:S(2)}, u32[]{:S(2)}) collective-permute-start(bf16[128,2,128]{2,1,0:T(2,128)(2,1)S(1)} %get-tuple-element.49), channel_id=1, source_target_pairs={{0,1},{2,3},{4,5},{6,7},{8,9},{10,11},{12,13},{14,15},{16,17},{18,... | collective-permute-start | bytes 196616 | tf_op jit(solution)/shard_map/ppermute | solution.py:10
  29.9 4.3 %collective-permute-start.5 = (bf16[128,2,128]{2,1,0:T(2,128)(2,1)S(1)}, bf16[128,2,128]{2,1,0:T(2,128)(2,1)S(1)}, u32[]{:S(2)}, u32[]{:S(2)}) collective-permute-start(bf16[128,2,128]{2,1,0:T(2,128)(2,1)S(1)} %get-tuple-element.46), channel_id=1, source_target_pairs={{1,0},{3,2},{5,4},{7,6},{9,8},{11,10},{13,12},{15,14},{17,16},{19,... | collective-permute-start | bytes 196616 | tf_op jit(solution)/shard_map/ppermute | solution.py:10
  36.0 0.7 copy-start
  37.8 17.7 %collective-permute-start.8 = (bf16[128,4,128]{2,1,0:T(4,128)(2,1)S(1)}, bf16[128,4,128]{2,1,0:T(4,128)(2,1)S(1)}, u32[]{:S(2)}, u32[]{:S(2)}) collective-permute-start(bf16[128,4,128]{2,1,0:T(4,128)(2,1)S(1)} %get-tuple-element.38), channel_id=1, source_target_pairs={{0,2},{2,4},{4,6},{1,3},{3,5},{5,7},{8,10},{10,12},{12,14},{9,11},... | collective-permute-start | bytes 393224 | tf_op jit(solution)/shard_map/ppermute | solution.py:10
  41.0 2.6 %slice-start = ((bf16[128,7,128]{2,1,0:T(8,128)(2,1)}), bf16[128,2,128]{2,1,0:T(2,128)(2,1)S(1)}, s32[]{:S(2)}) async-start(bf16[128,7,128]{2,1,0:T(8,128)(2,1)} %copy-done), calls=%async_computation.2 | async-start | bytes 131072 | tf_op jit(solution)/shard_map/slice | solution.py:23
  41.3 10.4 %collective-permute-start.6 = (bf16[128,4,128]{2,1,0:T(4,128)(2,1)S(1)}, bf16[128,4,128]{2,1,0:T(4,128)(2,1)S(1)}, u32[]{:S(2)}, u32[]{:S(2)}) collective-permute-start(bf16[128,4,128]{2,1,0:T(4,128)(2,1)S(1)} %fusion.45), channel_id=1, source_target_pairs={{0,8},{8,16},{16,24},{1,9},{9,17},{17,25},{2,10},{10,18},{18,26},{... | collective-permute-start | bytes 393224 | tf_op jit(solution)/shard_map/ppermute | solution.py:10
  43.7 11.7 %collective-permute-start.7 = (bf16[128,4,128]{2,1,0:T(4,128)(2,1)S(1)}, bf16[128,4,128]{2,1,0:T(4,128)(2,1)S(1)}, u32[]{:S(2)}, u32[]{:S(2)}) collective-permute-start(bf16[128,4,128]{2,1,0:T(4,128)(2,1)S(1)} %pad_maximum_fusion.11), channel_id=1, source_target_pairs={{8,0},{16,8},{24,16},{9,1},{17,9},{25,17},{10,2},{18,10},{26,18},{... | collective-permute-start | bytes 393224 | tf_op jit(solution)/shard_map/ppermute | solution.py:10
  47.7 7.9 %collective-permute-start.9 = (bf16[128,4,128]{2,1,0:T(4,128)(2,1)S(1)}, bf16[128,4,128]{2,1,0:T(4,128)(2,1)S(1)}, u32[]{:S(2)}, u32[]{:S(2)}) collective-permute-start(bf16[128,4,128]{2,1,0:T(4,128)(2,1)S(1)} %get-tuple-element.39), channel_id=1, source_target_pairs={{2,0},{4,2},{6,4},{3,1},{5,3},{7,5},{10,8},{12,10},{14,12},{11,9},... | collective-permute-start | bytes 393224 | tf_op jit(solution)/shard_map/ppermute | solution.py:10
  49.8 5.9 %collective-permute-start.10 = (bf16[128,4,128]{2,1,0:T(4,128)(2,1)S(1)}, bf16[128,4,128]{2,1,0:T(4,128)(2,1)S(1)}, u32[]{:S(2)}, u32[]{:S(2)}) collective-permute-start(bf16[128,4,128]{2,1,0:T(4,128)(2,1)S(1)} %get-tuple-element.40), channel_id=1, source_target_pairs={{0,1},{2,3},{4,5},{6,7},{8,9},{10,11},{12,13},{14,15},{16,17},{18,... | collective-permute-start | bytes 393224 | tf_op jit(solution)/shard_map/ppermute | solution.py:10
  51.7 4.4 %collective-permute-start.11 = (bf16[128,4,128]{2,1,0:T(4,128)(2,1)S(1)}, bf16[128,4,128]{2,1,0:T(4,128)(2,1)S(1)}, u32[]{:S(2)}, u32[]{:S(2)}) collective-permute-start(bf16[128,4,128]{2,1,0:T(4,128)(2,1)S(1)} %get-tuple-element.37), channel_id=1, source_target_pairs={{1,0},{3,2},{5,4},{7,6},{9,8},{11,10},{13,12},{15,14},{17,16},{19,... | collective-permute-start | bytes 393224 | tf_op jit(solution)/shard_map/ppermute | solution.py:10
  59.0 0.9 %copy-start.2 = (bf16[6,128,1,128]{1,3,0,2:T(8,128)(2,1)S(1)}, bf16[6,128,1,128]{1,3,0,2:T(8,128)(2,1)}, u32[]{:S(2)}) copy-start(bf16[6,128,1,128]{1,3,0,2:T(8,128)(2,1)} %copy.186) | copy-start | bytes 589828
  61.6 15.3 %collective-permute-start.12 = (bf16[128,2,128]{2,1,0:T(2,128)(2,1)S(1)}, bf16[128,2,128]{2,1,0:T(2,128)(2,1)S(1)}, u32[]{:S(2)}, u32[]{:S(2)}) collective-permute-start(bf16[128,2,128]{2,1,0:T(2,128)(2,1)S(1)} %get-tuple-element.45), channel_id=1, source_target_pairs={{0,8},{8,16},{16,24},{1,9},{9,17},{17,25},{2,10},{10,18},{18,26},{... | collective-permute-start | bytes 196616 | tf_op jit(solution)/shard_map/ppermute | solution.py:10
  64.0 0.8 copy-start.3
  66.1 14.3 %collective-permute-start.13 = (bf16[128,2,128]{2,1,0:T(2,128)(2,1)S(1)}, bf16[128,2,128]{2,1,0:T(2,128)(2,1)S(1)}, u32[]{:S(2)}, u32[]{:S(2)}) collective-permute-start(bf16[128,2,128]{2,1,0:T(2,128)(2,1)S(1)} %stack.190), channel_id=1, source_target_pairs={{8,0},{16,8},{24,16},{9,1},{17,9},{25,17},{10,2},{18,10},{26,18},{... | collective-permute-start | bytes 196616 | tf_op jit(solution)/shard_map/ppermute | solution.py:10
  70.3 10.1 %collective-permute-start.14 = (bf16[128,2,128]{2,1,0:T(2,128)(2,1)S(1)}, bf16[128,2,128]{2,1,0:T(2,128)(2,1)S(1)}, u32[]{:S(2)}, u32[]{:S(2)}) collective-permute-start(bf16[128,2,128]{2,1,0:T(2,128)(2,1)S(1)} %get-tuple-element.42), channel_id=1, source_target_pairs={{0,2},{2,4},{4,6},{1,3},{3,5},{5,7},{8,10},{10,12},{12,14},{9,11},... | collective-permute-start | bytes 196616 | tf_op jit(solution)/shard_map/ppermute | solution.py:10
  73.5 7.0 %collective-permute-start.15 = (bf16[128,2,128]{2,1,0:T(2,128)(2,1)S(1)}, bf16[128,2,128]{2,1,0:T(2,128)(2,1)S(1)}, u32[]{:S(2)}, u32[]{:S(2)}) collective-permute-start(bf16[128,2,128]{2,1,0:T(2,128)(2,1)S(1)} %get-tuple-element.43), channel_id=1, source_target_pairs={{2,0},{4,2},{6,4},{3,1},{5,3},{7,5},{10,8},{12,10},{14,12},{11,9},... | collective-permute-start | bytes 196616 | tf_op jit(solution)/shard_map/ppermute | solution.py:10
  75.6 5.0 %collective-permute-start.16 = (bf16[128,2,128]{2,1,0:T(2,128)(2,1)S(1)}, bf16[128,2,128]{2,1,0:T(2,128)(2,1)S(1)}, u32[]{:S(2)}, u32[]{:S(2)}) collective-permute-start(bf16[128,2,128]{2,1,0:T(2,128)(2,1)S(1)} %get-tuple-element.44), channel_id=1, source_target_pairs={{0,1},{2,3},{4,5},{6,7},{8,9},{10,11},{12,13},{14,15},{16,17},{18,... | collective-permute-start | bytes 196616 | tf_op jit(solution)/shard_map/ppermute | solution.py:10
  77.0 4.3 %collective-permute-start.17 = (bf16[128,2,128]{2,1,0:T(2,128)(2,1)S(1)}, bf16[128,2,128]{2,1,0:T(2,128)(2,1)S(1)}, u32[]{:S(2)}, u32[]{:S(2)}) collective-permute-start(bf16[128,2,128]{2,1,0:T(2,128)(2,1)S(1)} %get-tuple-element.41), channel_id=1, source_target_pairs={{1,0},{3,2},{5,4},{7,6},{9,8},{11,10},{13,12},{15,14},{17,16},{19,... | collective-permute-start | bytes 196616 | tf_op jit(solution)/shard_map/ppermute | solution.py:10
  81.9 1.0 %copy-start.1 = (bf16[128,7,128]{2,1,0:T(8,128)(2,1)S(1)}, bf16[128,7,128]{2,1,0:T(8,128)(2,1)}, u32[]{:S(2)}) copy-start(bf16[128,7,128]{2,1,0:T(8,128)(2,1)} %copy-done) | copy-start | bytes 688132
where the time goes:
time: 85 us; the launch traced here: 84.2 us
  starting transfers between devices  55.9 us (66%)
  local copies, waits for them, and re-layouts  13.5 us (16%)
  other arithmetic  7.53 us (9%)
  matrix products  3.26 us (4%)
  between operations  2.05 us (2%)
  waiting for transfers between devices  1.86 us (2%)
    ppermute x18, starting transfers between devices, from_behind(): return lax.ppermute(x, axis, pairs)  48.6 us
    unnamed x35, local copies, waits for them, and re-layouts  5.51 us
    all_to_all x1, starting transfers between devices, body(): lax.all_to_all(label_out, 'gz', split_axis=0, concat_axis=0, tiled=True)  3.86 us
    all_to_all x1, starting transfers between devices, body(): lax.all_to_all(outgoing, 'gz', split_axis=0, concat_axis=0, tiled=True)  3.47 us
    slice x3, local copies, waits for them, and re-layouts, block_product(): halo[:, :, 1, :]  2.81 us
    another operation x5, other arithmetic, packed(): jnp.stack([matrix[:, which_block, :] for matrix in matrices for which_blo...  2.47 us
  transfers between devices with their start and end apart: 20, of which 4 were waited for; matrix products, arithmetic and copies ran while one was open for 10% of the time, Pallas kernels for 0%

commit v1 on v0

v1 whole, which is shorter than its diff:
```python
import functools

import jax
import jax.numpy as jnp
from jax import lax
from jax.experimental import pallas as pl
from jax.experimental.pallas import tpu as pltpu
from jax.sharding import PartitionSpec as P

AXES = ("gx", "gy", "gz")
PARTS = 7
LINKS = ("xa", "xb", "ya", "yb", "z")


def even_partner(i, n):
    j = i ^ 1
    return j if j < n else None


def odd_partner(i, n):
    j = i + 1 if i % 2 else i - 1
    return j if 0 <= j < n else None


def swap_pairs(sizes, link):
    nx, ny, nz = sizes
    pairs = []
    for x in range(nx):
        for y in range(ny):
            for z in range(nz):
                to = None
                if link[0] == "x":
                    near = (even_partner if link == "xa" else odd_partner)(x, nx)
                    to = None if near is None else (near, y, z)
                elif link[0] == "y":
                    near = (even_partner if link == "ya" else odd_partner)(y, ny)
                    to = None if near is None else (x, near, z)
                if to is None:
                    to = (x, y, z ^ 1)
                pairs.append(((x * ny + y) * nz + z, (to[0] * ny + to[1]) * nz + to[2]))
    return pairs


def place(sizes):
    nx, ny, nz = sizes
    x, y, z = (lax.axis_index(a) for a in AXES)
    slots, valids = [], []
    for pos, n, base in ((x, nx, 1), (y, ny, 3)):
        odd = pos % 2
        slots += [base + 1 - odd, base + odd]
        valids += [(odd == 1) | (pos + 1 < n), jnp.where(odd == 1, pos + 1 < n, pos > 0)]
    slots.append(6 - z)
    valids.append(z >= 0)
    return slots, valids


def eye_scaled(size, dtype=jnp.float32):
    rows = lax.broadcasted_iota(jnp.int32, (size, size), 0)
    cols = lax.broadcasted_iota(jnp.int32, (size, size), 1)
    return jnp.where(rows == cols, jnp.asarray(1.5, dtype), jnp.asarray(0.0, dtype))


def keep(flag, block):
    return jnp.where(flag, block, jnp.zeros_like(block))


def mm(a, b):
    return jnp.dot(a, b, preferred_element_type=jnp.float32)


def half(block):
    return (block.astype(jnp.float32) * -0.5).astype(jnp.bfloat16)


def corrected(eye, block):
    return (eye - 0.5 * block.astype(jnp.float32)).astype(jnp.bfloat16)


def place_kernel(sizes, own_cols, other_cols, home, ypat, zpat, own, other, row, *messages):
    count, size = own.shape[1], own.shape[2]
    slots, valids = place(sizes)
    moved = home[0] != lax.axis_index("gz")
    cols = [jnp.where(moved, other_cols[0, k], own_cols[0, k]) for k in range(count)]

    def pick(slot, valid):
        index = jnp.int32(0)
        found = jnp.bool_(False)
        for k in range(count):
            hit = cols[k] == slot
            index = jnp.where(hit, k, index)
            found = found | hit
        block = jnp.where(moved, other[0, index], own[0, index])
        return keep(found & valid, block)

    diag = pick(jnp.int32(0), jnp.bool_(True))
    row[0] = diag
    for q, message in enumerate(messages):
        slot, valid = slots[q], valids[q]
        block = pick(slot, valid)
        row[q + 1] = block
        message[0:size] = diag
        message[size : 2 * size] = keep(ypat[0, slot] == 1, block)
        flag = jnp.where(zpat[0, slot] == 1, 1.0, 0.0)
        message[2 * size :] = jnp.full((message.shape[0] - 2 * size, size), flag, jnp.bfloat16)


def unpack(message, size, valid):
    return message[0:size], keep(valid, message[size : 2 * size])


def diagonal_kernel(sizes, ypat, zpat, row, *refs):
    n = len(LINKS)
    messages, packed, ycol = refs[:n], refs[n], refs[n + 1]
    size = row.shape[1]
    slots, valids = place(sizes)
    eye = eye_scaled(size)
    diag = row[0]
    t0 = corrected(eye, diag)
    total = mm(diag, t0)
    cols = []
    for q in range(n):
        near_diag, facing = unpack(messages[q], size, valids[q])
        tfacing = half(facing)
        total += mm(row[q + 1], tfacing)
        col = (mm(near_diag, tfacing) + mm(facing, t0)).astype(jnp.bfloat16)
        ycol[q] = col
        cols.append(col)
    y0 = total.astype(jnp.bfloat16)
    quad = mm(t0, y0)
    for q in range(n):
        both = (ypat[0, slots[q]] == 1) & (zpat[0, slots[q]] == 1)
        quad += mm(half(keep(both, row[q + 1])), cols[q])
    packed[0:size] = y0
    packed[size:] = (eye - 0.5 * quad).astype(jnp.bfloat16)


def between_kernel(sizes, ypat, row, packed, ycol, *refs):
    n = len(LINKS)
    messages, yrow, yown = refs[:n], refs[n], refs[n + 1]
    size = row.shape[1]
    slots, valids = place(sizes)
    eye = eye_scaled(size)
    diag, y0, tm0 = row[0], packed[0:size], packed[size:]
    total = mm(y0, tm0)
    for q in range(n):
        near_diag, facing = unpack(messages[q], size, valids[q])
        near_t = corrected(eye, near_diag)
        kept = ypat[0, slots[q]] == 1
        block = row[q + 1]
        y1 = keep(kept, (mm(diag, half(block)) + mm(block, near_t)).astype(jnp.bfloat16))
        yrow[q] = y1
        zflag = messages[q][2 * size : 2 * size + 1, 0:1] > 0
        zfacing = jnp.where(zflag, half(facing), jnp.zeros_like(facing))
        quad = mm(near_t, ycol[q]) + mm(zfacing, y0)
        total += mm(y1, (-0.5 * quad).astype(jnp.bfloat16))
    yown[...] = total.astype(jnp.bfloat16)


def last_kernel(sizes, ypat, zpat, row, packed, yrow, yown, *refs):
    n = len(LINKS)
    messages, arrived, zout, yout = refs[:n], refs[n : 2 * n], refs[2 * n], refs[2 * n + 1]
    size = row.shape[1]
    slots, valids = place(sizes)
    eye = eye_scaled(size)
    y0, tm0 = packed[0:size], packed[size:]
    t0 = corrected(eye, row[0])
    total = mm(tm0, t0)
    for q in range(n):
        slot = slots[q]
        kept_y = ypat[0, slot] == 1
        kept_z = zpat[0, slot] == 1
        near_diag, facing = unpack(messages[q], size, valids[q])
        near_t = corrected(eye, near_diag)
        near_y, near_tm = arrived[q][0:size], arrived[q][size:]
        zrow = half(keep(kept_y & kept_z, row[q + 1]))
        y1 = yrow[q]
        quad = mm(t0, y1) + mm(zrow, near_y)
        tm = keep(kept_y & valids[q], (-0.5 * quad).astype(jnp.bfloat16))
        yout[slot] = keep(
            kept_y & valids[q], (mm(y0, tm) + mm(y1, near_tm)).astype(jnp.bfloat16)
        )
        zout[slot] = keep(
            kept_z & valids[q], (mm(tm0, zrow) + mm(tm, near_t)).astype(jnp.bfloat16)
        )
        zflag = messages[q][2 * size : 2 * size + 1, 0:1] > 0
        total += mm(tm, jnp.where(zflag, half(facing), jnp.zeros_like(facing)))
    absent = 11 - slots[-1]
    zout[absent] = jnp.zeros((size, size), jnp.bfloat16)
    yout[absent] = jnp.zeros((size, size), jnp.bfloat16)
    zout[0] = total.astype(jnp.bfloat16)
    yout[0] = yown[...]


def call(kernel, out_shapes, smem, vmem):
    vspec = pl.BlockSpec(memory_space=pltpu.VMEM)
    return pl.pallas_call(
        kernel,
        out_shape=[jax.ShapeDtypeStruct(s, jnp.bfloat16) for s in out_shapes],
        in_specs=[pl.BlockSpec(memory_space=pltpu.SMEM)] * len(smem) + [vspec] * len(vmem),
        out_specs=[vspec] * len(out_shapes),
    )(*smem, *vmem)


def body(sizes, s_blocks, s_columns, new_home, z_pattern, y_pattern):
    size = s_blocks.shape[2]
    n = len(LINKS)
    pairs = {link: swap_pairs(sizes, link) for link in LINKS}

    def send(x, link):
        return lax.ppermute(x, AXES, pairs[link])

    other = send(s_blocks, "z")
    other_cols = send(s_columns, "z")
    row, *messages = call(
        functools.partial(place_kernel, sizes),
        [(n + 1, size, size)] + [(2 * size + 16, size)] * n,
        [s_columns, other_cols, new_home, y_pattern, z_pattern],
        [s_blocks, other],
    )
    messages = [send(m, link) for m, link in zip(messages, LINKS)]
    packed, ycol = call(
        functools.partial(diagonal_kernel, sizes),
        [(2 * size, size), (n, size, size)],
        [y_pattern, z_pattern],
        [row, *messages],
    )
    arrived = [send(packed, link) for link in LINKS]
    yrow, yown = call(
        functools.partial(between_kernel, sizes),
        [(n, size, size), (size, size)],
        [y_pattern],
        [row, packed, ycol, *messages],
    )
    zout, yout = call(
        functools.partial(last_kernel, sizes),
        [(PARTS, size, size)] * 2,
        [y_pattern, z_pattern],
        [row, packed, yrow, yown, *messages, *arrived],
    )
    return tuple(jnp.transpose(o, (1, 0, 2))[None] for o in (zout, yout))


def solution(mesh):
    sizes = tuple(mesh.shape[a] for a in AXES)
    in_specs = (
        P(AXES, None, None, None),
        P(AXES, None),
        P(AXES),
        P(AXES, None),
        P(AXES, None),
    )
    out_specs = (P(AXES, None, None, None), P(AXES, None, None, None))
    return jax.shard_map(
        functools.partial(body, sizes),
        mesh=mesh,
        in_specs=in_specs,
        out_specs=out_specs,
        check_vma=False,
    )
```

time: 85 us -> 31.4 us (0.37)
  the two profiles are of different devices: /device:TPU:13 before, /device:TPU:0 now
where the time goes in v1:
time: 31.4 us; the launch traced here: 31.2 us
  starting transfers between devices  13.4 us (43%)
  Pallas kernels  9.96 us (32%)
  waiting for transfers between devices  4.01 us (13%)
  local copies, waits for them, and re-layouts  2.44 us (8%)
  between operations  1.39 us (4%)
    ppermute x12, starting transfers between devices, send(): return lax.ppermute(x, AXES, pairs[link])  13.4 us
    pallas_call x4, Pallas kernels, call(): pl.pallas_call(kernel, out_shape=[jax.ShapeDtypeStruct(s, jnp.bfloat16) f...  9.96 us
    ppermute x12, waiting for transfers between devices, send(): return lax.ppermute(x, AXES, pairs[link])  4.01 us
    unnamed x24, local copies, waits for them, and re-layouts  2.44 us
  transfers between devices with their start and end apart: 12, of which 4 were waited for; matrix products, arithmetic and copies ran while one was open for 0% of the time, Pallas kernels for 9%

profile of v1, /device:TPU:0, one launch (start us, length us, event | category | flops | bytes accessed | tf_op | source)
XLA Modules:
  0.0 31.2 jit_solution(10998077621829717340)
XLA Ops:
  0.6 0.6 %collective-permute-start.1 = (bf16[1,4,128,128]{3,2,1,0:T(8,128)(2,1)}, bf16[1,4,128,128]{3,2,1,0:T(8,128)(2,1)S(1)}, u32[]{:S(2)}, u32[]{:S(2)}) collective-permute-start(bf16[1,4,128,128]{3,2,1,0:T(8,128)(2,1)} %own.1), channel_id=1, source_target_pairs={{0,1},{1,0},{2,3},{3,2},{4,5},{5,4},{6,7},{7,6},{8,9},{9,8},{10,11... | collective-permute-start | bytes 393224 | tf_op jit(solution)/shard_map/ppermute | solution.py:210
  1.2 0.1 collective-permute-start
  1.9 0.6 %collective-permute-done.other_cols = s32[1,4]{1,0:T(1,128)S(1)} collective-permute-done((s32[1,4]{1,0:T(1,128)}, s32[1,4]{1,0:T(1,128)S(1)}, u32[]{:S(2)}, u32[]{:S(2)}) %collective-permute-start) | collective-permute-done | bytes 48 | tf_op jit(solution)/shard_map/ppermute | solution.py:210
  2.5 0.0 copy-start.11
  2.5 0.0 collective-permute-done.1.other
  2.5 0.5 %copy-done.11 = s32[1,4]{1,0:T(1,128)} copy-done((s32[1,4]{1,0:T(1,128)}, s32[1,4]{1,0:T(1,128)S(1)}, u32[]{:S(2)}) %copy-start.11) | copy-done | bytes 40
  3.0 0.0 copy-start.5
  3.0 0.7 %copy-done.5 = bf16[1,4,128,128]{3,2,1,0:T(8,128)(2,1)} copy-done((bf16[1,4,128,128]{3,2,1,0:T(8,128)(2,1)}, bf16[1,4,128,128]{3,2,1,0:T(8,128)(2,1)S(1)}, u32[]{:S(2)}) %copy-start.5) | copy-done | bytes 131096
  3.7 1.9 %shard_map.68 = (bf16[6,128,128]{2,1,0:T(8,128)(2,1)}, bf16[272,128]{1,0:T(8,128)(2,1)}, bf16[272,128]{1,0:T(8,128)(2,1)}, bf16[272,128]{1,0:T(8,128)(2,1)}, bf1...) custom-call(s32[1,4]{1,0:T(1,128)} %own_cols.1, s32[1,4]{1,0:T(1,128)} %copy-done.11, s32[1]{0:T(128)S(6)} %copy.7.home, ...), custom_call_target="tpu_custom_call" | custom-call | tf_op jit(solution)/shard_map/pallas_call | solution.py:196
  5.6 2.7 %collective-permute-start.2 = (bf16[272,128]{1,0:T(8,128)(2,1)}, bf16[272,128]{1,0:T(8,128)(2,1)S(1)}, u32[]{:S(2)}, u32[]{:S(2)}) collective-permute-start(bf16[272,128]{1,0:T(8,128)(2,1)} %get-tuple-element.15), channel_id=1, source_target_pairs={{0,8},{1,9},{2,10},{3,11},{4,12},{5,13},{6,14},{7,15},{8,0},{9,1},... | collective-permute-start | bytes 208904 | tf_op jit(solution)/shard_map/ppermute | solution.py:210
  8.3 0.0 collective-permute-start.3
  8.3 1.6 %collective-permute-start.4 = (bf16[272,128]{1,0:T(8,128)(2,1)}, bf16[272,128]{1,0:T(8,128)(2,1)S(1)}, u32[]{:S(2)}, u32[]{:S(2)}) collective-permute-start(bf16[272,128]{1,0:T(8,128)(2,1)} %get-tuple-element.17), channel_id=1, source_target_pairs={{0,2},{1,3},{2,0},{3,1},{4,6},{5,7},{6,4},{7,5},{8,10},{9,11},{10,... | collective-permute-start | bytes 208904 | tf_op jit(solution)/shard_map/ppermute | solution.py:210
  9.9 0.2 collective-permute-start.5
  10.1 0.3 collective-permute-start.6
  10.4 0.7 %collective-permute-done.2.refs_0_ = bf16[272,128]{1,0:T(8,128)(2,1)S(1)} collective-permute-done((bf16[272,128]{1,0:T(8,128)(2,1)}, bf16[272,128]{1,0:T(8,128)(2,1)S(1)}, u32[]{:S(2)}, u32[]{:S(2)}) %collective-permute-start.2) | collective-permute-done | bytes 69664 | tf_op jit(solution)/shard_map/ppermute | solution.py:210
  11.1 0.0 copy-start
  11.1 0.0 collective-permute-done.3.refs_1_
  11.1 0.0 copy-start.1
  11.1 2.0 %collective-permute-done.4.refs_2_ = bf16[272,128]{1,0:T(8,128)(2,1)S(1)} collective-permute-done((bf16[272,128]{1,0:T(8,128)(2,1)}, bf16[272,128]{1,0:T(8,128)(2,1)S(1)}, u32[]{:S(2)}, u32[]{:S(2)}) %collective-permute-start.4) | collective-permute-done | bytes 69664 | tf_op jit(solution)/shard_map/ppermute | solution.py:210
  13.1 0.0 copy-start.2
  13.1 0.0 collective-permute-done.5.refs_3_
  13.1 0.0 copy-start.3
  13.1 0.0 collective-permute-done.6.refs_4_
  13.1 0.0 copy-start.4
  13.1 0.0 copy-done
  13.2 0.0 copy-done.1
  13.2 0.6 %copy-done.2 = bf16[272,128]{1,0:T(8,128)(2,1)} copy-done((bf16[272,128]{1,0:T(8,128)(2,1)}, bf16[272,128]{1,0:T(8,128)(2,1)S(1)}, u32[]{:S(2)}) %copy-start.2) | copy-done | bytes 69656
  13.8 0.0 copy-done.3
  13.8 0.0 copy-done.4
  13.8 2.3 %shard_map.69 = (bf16[256,128]{1,0:T(8,128)(2,1)}, bf16[5,128,128]{2,1,0:T(8,128)(2,1)}) custom-call(s32[1,7]{1,0:T(1,128)} %ypat.7, s32[1,7]{1,0:T(1,128)} %zpat.5, bf16[6,128,128]{2,1,0:T(8,128)(2,1)} %get-tuple-element.14.row, bf16[272,128]{1,0:T(8,128)(2,1)} %copy-done, bf16[272,128]{1,0:T(8,128)(2,1)} %copy-done.1, bf16[272,128]{1,0:T(8,128)(2,1)} %copy-done.2, ...), custom_call_target="tpu_custom_call" | custom-call | tf_op jit(solution)/shard_map/pallas_call | solution.py:196
  16.1 0.0 collective-permute-start.11
  16.1 0.5 %collective-permute-start.10 = (bf16[256,128]{1,0:T(8,128)(2,1)}, bf16[256,128]{1,0:T(8,128)(2,1)S(1)}, u32[]{:S(2)}, u32[]{:S(2)}) collective-permute-start(bf16[256,128]{1,0:T(8,128)(2,1)} %get-tuple-element.20.packed), channel_id=1, source_target_pairs={{0,1},{1,0},{2,4},{3,5},{4,2},{5,3},{6,7},{7,6},{8,9},{9,8},{10,12... | collective-permute-start | bytes 196616 | tf_op jit(solution)/shard_map/ppermute | solution.py:210
  16.6 4.0 %collective-permute-start.9 = (bf16[256,128]{1,0:T(8,128)(2,1)}, bf16[256,128]{1,0:T(8,128)(2,1)S(1)}, u32[]{:S(2)}, u32[]{:S(2)}) collective-permute-start(bf16[256,128]{1,0:T(8,128)(2,1)} %get-tuple-element.20.packed), channel_id=1, source_target_pairs={{0,2},{1,3},{2,0},{3,1},{4,6},{5,7},{6,4},{7,5},{8,10},{9,11},{10,... | collective-permute-start | bytes 196616 | tf_op jit(solution)/shard_map/ppermute | solution.py:210
  20.5 0.0 collective-permute-start.8
  20.5 3.5 %collective-permute-start.7 = (bf16[256,128]{1,0:T(8,128)(2,1)}, bf16[256,128]{1,0:T(8,128)(2,1)S(1)}, u32[]{:S(2)}, u32[]{:S(2)}) collective-permute-start(bf16[256,128]{1,0:T(8,128)(2,1)} %get-tuple-element.20.packed), channel_id=1, source_target_pairs={{0,8},{1,9},{2,10},{3,11},{4,12},{5,13},{6,14},{7,15},{8,0},{9,1},... | collective-permute-start | bytes 196616 | tf_op jit(solution)/shard_map/ppermute | solution.py:210
  24.0 2.7 %shard_map.70 = (bf16[5,128,128]{2,1,0:T(8,128)(2,1)}, bf16[128,128]{1,0:T(8,128)(2,1)}) custom-call(s32[1,7]{1,0:T(1,128)} %ypat.7, bf16[6,128,128]{2,1,0:T(8,128)(2,1)} %get-tuple-element.14.row, bf16[256,128]{1,0:T(8,128)(2,1)} %get-tuple-element.20.packed, bf16[5,128,128]{2,1,0:T(8,128)(2,1)} %get-tuple-element.21.ycol, bf16[272,128]{1,0:T(8,128)(2,1)} %copy-done, ...), custom_call_target="tpu_custom_call" | custom-call | tf_op jit(solution)/shard_map/pallas_call | solution.py:196
  26.7 0.0 collective-permute-done.11.refs_9_
  26.7 0.0 copy-start.6
  26.7 0.0 collective-permute-done.10.refs_8_
  26.7 0.0 copy-start.7
  26.7 0.0 collective-permute-done.9.refs_7_
  26.7 0.0 copy-start.8
  26.7 0.0 collective-permute-done.8.refs_6_
  26.7 0.0 copy-start.9
  26.8 0.7 %collective-permute-done.7.refs_5_ = bf16[256,128]{1,0:T(8,128)(2,1)S(1)} collective-permute-done((bf16[256,128]{1,0:T(8,128)(2,1)}, bf16[256,128]{1,0:T(8,128)(2,1)S(1)}, u32[]{:S(2)}, u32[]{:S(2)}) %collective-permute-start.7) | collective-permute-done | bytes 65568 | tf_op jit(solution)/shard_map/ppermute | solution.py:210
  27.5 0.0 copy-start.10
  27.5 0.0 copy-done.6
  27.5 0.0 copy-done.7
  27.5 0.0 copy-done.8
  27.5 0.0 copy-done.9
  27.5 0.6 %copy-done.10 = bf16[256,128]{1,0:T(8,128)(2,1)} copy-done((bf16[256,128]{1,0:T(8,128)(2,1)}, bf16[256,128]{1,0:T(8,128)(2,1)S(1)}, u32[]{:S(2)}) %copy-start.10) | copy-done | bytes 65560
  28.1 3.1 %shard_map.71 = (bf16[7,128,128]{2,1,0:T(8,128)(2,1)}, bf16[7,128,128]{2,1,0:T(8,128)(2,1)}) custom-call(s32[1,7]{1,0:T(1,128)} %ypat.7, s32[1,7]{1,0:T(1,128)} %zpat.5, bf16[6,128,128]{2,1,0:T(8,128)(2,1)} %get-tuple-element.14.row, bf16[256,128]{1,0:T(8,128)(2,1)} %get-tuple-element.20.packed, bf16[5,128,128]{2,1,0:T(8,128)(2,1)} %get-tuple-element.22.yrow, ...), custom_call_target="tpu_custom_call" | custom-call | tf_op jit(solution)/shard_map/pallas_call | solution.py:196
Async XLA Ops:
  0.6 1.9 %collective-permute-start.1 = (bf16[1,4,128,128]{3,2,1,0:T(8,128)(2,1)}, bf16[1,4,128,128]{3,2,1,0:T(8,128)(2,1)S(1)}, u32[]{:S(2)}, u32[]{:S(2)}) collective-permute-start(bf16[1,4,128,128]{3,2,1,0:T(8,128)(2,1)} %own.1), channel_id=1, source_target_pairs={{0,1},{1,0},{2,3},{3,2},{4,5},{5,4},{6,7},{7,6},{8,9},{9,8},{10,11... | collective-permute-start | bytes 393224 | tf_op jit(solution)/shard_map/ppermute | solution.py:210
  1.2 1.3 %collective-permute-start = (s32[1,4]{1,0:T(1,128)}, s32[1,4]{1,0:T(1,128)S(1)}, u32[]{:S(2)}, u32[]{:S(2)}) collective-permute-start(s32[1,4]{1,0:T(1,128)} %own_cols.1), channel_id=1, source_target_pairs={{0,1},{1,0},{2,3},{3,2},{4,5},{5,4},{6,7},{7,6},{8,9},{9,8},{10,11... | collective-permute-start | bytes 56 | tf_op jit(solution)/shard_map/ppermute | solution.py:210
  2.5 0.5 %copy-start.11 = (s32[1,4]{1,0:T(1,128)}, s32[1,4]{1,0:T(1,128)S(1)}, u32[]{:S(2)}) copy-start(s32[1,4]{1,0:T(1,128)S(1)} %collective-permute-done.other_cols) | copy-start | bytes 52
  3.0 0.7 %copy-start.5 = (bf16[1,4,128,128]{3,2,1,0:T(8,128)(2,1)}, bf16[1,4,128,128]{3,2,1,0:T(8,128)(2,1)S(1)}, u32[]{:S(2)}) copy-start(bf16[1,4,128,128]{3,2,1,0:T(8,128)(2,1)S(1)} %collective-permute-done.1.other) | copy-start | bytes 393220
  5.6 5.5 %collective-permute-start.2 = (bf16[272,128]{1,0:T(8,128)(2,1)}, bf16[272,128]{1,0:T(8,128)(2,1)S(1)}, u32[]{:S(2)}, u32[]{:S(2)}) collective-permute-start(bf16[272,128]{1,0:T(8,128)(2,1)} %get-tuple-element.15), channel_id=1, source_target_pairs={{0,8},{1,9},{2,10},{3,11},{4,12},{5,13},{6,14},{7,15},{8,0},{9,1},... | collective-permute-start | bytes 208904 | tf_op jit(solution)/shard_map/ppermute | solution.py:210
  8.3 2.8 %collective-permute-start.3 = (bf16[272,128]{1,0:T(8,128)(2,1)}, bf16[272,128]{1,0:T(8,128)(2,1)S(1)}, u32[]{:S(2)}, u32[]{:S(2)}) collective-permute-start(bf16[272,128]{1,0:T(8,128)(2,1)} %get-tuple-element.16), channel_id=1, source_target_pairs={{0,1},{1,0},{2,3},{3,2},{4,5},{5,4},{6,7},{7,6},{8,16},{9,17},{10,... | collective-permute-start | bytes 208904 | tf_op jit(solution)/shard_map/ppermute | solution.py:210
  8.3 4.8 %collective-permute-start.4 = (bf16[272,128]{1,0:T(8,128)(2,1)}, bf16[272,128]{1,0:T(8,128)(2,1)S(1)}, u32[]{:S(2)}, u32[]{:S(2)}) collective-permute-start(bf16[272,128]{1,0:T(8,128)(2,1)} %get-tuple-element.17), channel_id=1, source_target_pairs={{0,2},{1,3},{2,0},{3,1},{4,6},{5,7},{6,4},{7,5},{8,10},{9,11},{10,... | collective-permute-start | bytes 208904 | tf_op jit(solution)/shard_map/ppermute | solution.py:210
  9.9 3.2 %collective-permute-start.5 = (bf16[272,128]{1,0:T(8,128)(2,1)}, bf16[272,128]{1,0:T(8,128)(2,1)S(1)}, u32[]{:S(2)}, u32[]{:S(2)}) collective-permute-start(bf16[272,128]{1,0:T(8,128)(2,1)} %get-tuple-element.18), channel_id=1, source_target_pairs={{0,1},{1,0},{2,4},{3,5},{4,2},{5,3},{6,7},{7,6},{8,9},{9,8},{10,12... | collective-permute-start | bytes 208904 | tf_op jit(solution)/shard_map/ppermute | solution.py:210
  10.1 3.0 %collective-permute-start.6 = (bf16[272,128]{1,0:T(8,128)(2,1)}, bf16[272,128]{1,0:T(8,128)(2,1)S(1)}, u32[]{:S(2)}, u32[]{:S(2)}) collective-permute-start(bf16[272,128]{1,0:T(8,128)(2,1)} %get-tuple-element.19), channel_id=1, source_target_pairs={{0,1},{1,0},{2,3},{3,2},{4,5},{5,4},{6,7},{7,6},{8,9},{9,8},{10,11... | collective-permute-start | bytes 208904 | tf_op jit(solution)/shard_map/ppermute | solution.py:210
  11.1 2.0 %copy-start = (bf16[272,128]{1,0:T(8,128)(2,1)}, bf16[272,128]{1,0:T(8,128)(2,1)S(1)}, u32[]{:S(2)}) copy-start(bf16[272,128]{1,0:T(8,128)(2,1)S(1)} %collective-permute-done.2.refs_0_) | copy-start | bytes 208900
  11.1 2.0 %copy-start.1 = (bf16[272,128]{1,0:T(8,128)(2,1)}, bf16[272,128]{1,0:T(8,128)(2,1)S(1)}, u32[]{:S(2)}) copy-start(bf16[272,128]{1,0:T(8,128)(2,1)S(1)} %collective-permute-done.3.refs_1_) | copy-start | bytes 208900
  13.1 0.6 %copy-start.2 = (bf16[272,128]{1,0:T(8,128)(2,1)}, bf16[272,128]{1,0:T(8,128)(2,1)S(1)}, u32[]{:S(2)}) copy-start(bf16[272,128]{1,0:T(8,128)(2,1)S(1)} %collective-permute-done.4.refs_2_) | copy-start | bytes 208900
  13.1 0.7 %copy-start.3 = (bf16[272,128]{1,0:T(8,128)(2,1)}, bf16[272,128]{1,0:T(8,128)(2,1)S(1)}, u32[]{:S(2)}) copy-start(bf16[272,128]{1,0:T(8,128)(2,1)S(1)} %collective-permute-done.5.refs_3_) | copy-start | bytes 208900
  13.1 0.7 %copy-start.4 = (bf16[272,128]{1,0:T(8,128)(2,1)}, bf16[272,128]{1,0:T(8,128)(2,1)S(1)}, u32[]{:S(2)}) copy-start(bf16[272,128]{1,0:T(8,128)(2,1)S(1)} %collective-permute-done.6.refs_4_) | copy-start | bytes 208900
  16.1 10.6 %collective-permute-start.11 = (bf16[256,128]{1,0:T(8,128)(2,1)}, bf16[256,128]{1,0:T(8,128)(2,1)S(1)}, u32[]{:S(2)}, u32[]{:S(2)}) collective-permute-start(bf16[256,128]{1,0:T(8,128)(2,1)} %get-tuple-element.20.packed), channel_id=1, source_target_pairs={{0,1},{1,0},{2,3},{3,2},{4,5},{5,4},{6,7},{7,6},{8,9},{9,8},{10,11... | collective-permute-start | bytes 196616 | tf_op jit(solution)/shard_map/ppermute | solution.py:210
  16.1 10.6 %collective-permute-start.10 = (bf16[256,128]{1,0:T(8,128)(2,1)}, bf16[256,128]{1,0:T(8,128)(2,1)S(1)}, u32[]{:S(2)}, u32[]{:S(2)}) collective-permute-start(bf16[256,128]{1,0:T(8,128)(2,1)} %get-tuple-element.20.packed), channel_id=1, source_target_pairs={{0,1},{1,0},{2,4},{3,5},{4,2},{5,3},{6,7},{7,6},{8,9},{9,8},{10,12... | collective-permute-start | bytes 196616 | tf_op jit(solution)/shard_map/ppermute | solution.py:210
  16.6 10.1 %collective-permute-start.9 = (bf16[256,128]{1,0:T(8,128)(2,1)}, bf16[256,128]{1,0:T(8,128)(2,1)S(1)}, u32[]{:S(2)}, u32[]{:S(2)}) collective-permute-start(bf16[256,128]{1,0:T(8,128)(2,1)} %get-tuple-element.20.packed), channel_id=1, source_target_pairs={{0,2},{1,3},{2,0},{3,1},{4,6},{5,7},{6,4},{7,5},{8,10},{9,11},{10,... | collective-permute-start | bytes 196616 | tf_op jit(solution)/shard_map/ppermute | solution.py:210
  20.5 6.2 %collective-permute-start.8 = (bf16[256,128]{1,0:T(8,128)(2,1)}, bf16[256,128]{1,0:T(8,128)(2,1)S(1)}, u32[]{:S(2)}, u32[]{:S(2)}) collective-permute-start(bf16[256,128]{1,0:T(8,128)(2,1)} %get-tuple-element.20.packed), channel_id=1, source_target_pairs={{0,1},{1,0},{2,3},{3,2},{4,5},{5,4},{6,7},{7,6},{8,16},{9,17},{10,... | collective-permute-start | bytes 196616 | tf_op jit(solution)/shard_map/ppermute | solution.py:210
  20.5 6.9 %collective-permute-start.7 = (bf16[256,128]{1,0:T(8,128)(2,1)}, bf16[256,128]{1,0:T(8,128)(2,1)S(1)}, u32[]{:S(2)}, u32[]{:S(2)}) collective-permute-start(bf16[256,128]{1,0:T(8,128)(2,1)} %get-tuple-element.20.packed), channel_id=1, source_target_pairs={{0,8},{1,9},{2,10},{3,11},{4,12},{5,13},{6,14},{7,15},{8,0},{9,1},... | collective-permute-start | bytes 196616 | tf_op jit(solution)/shard_map/ppermute | solution.py:210
  26.7 0.8 %copy-start.6 = (bf16[256,128]{1,0:T(8,128)(2,1)}, bf16[256,128]{1,0:T(8,128)(2,1)S(1)}, u32[]{:S(2)}) copy-start(bf16[256,128]{1,0:T(8,128)(2,1)S(1)} %collective-permute-done.11.refs_9_) | copy-start | bytes 196612
  26.7 0.8 %copy-start.7 = (bf16[256,128]{1,0:T(8,128)(2,1)}, bf16[256,128]{1,0:T(8,128)(2,1)S(1)}, u32[]{:S(2)}) copy-start(bf16[256,128]{1,0:T(8,128)(2,1)S(1)} %collective-permute-done.10.refs_8_) | copy-start | bytes 196612
  26.7 0.8 %copy-start.8 = (bf16[256,128]{1,0:T(8,128)(2,1)}, bf16[256,128]{1,0:T(8,128)(2,1)S(1)}, u32[]{:S(2)}) copy-start(bf16[256,128]{1,0:T(8,128)(2,1)S(1)} %collective-permute-done.9.refs_7_) | copy-start | bytes 196612
  26.7 0.7 %copy-start.9 = (bf16[256,128]{1,0:T(8,128)(2,1)}, bf16[256,128]{1,0:T(8,128)(2,1)S(1)}, u32[]{:S(2)}) copy-start(bf16[256,128]{1,0:T(8,128)(2,1)S(1)} %collective-permute-done.8.refs_6_) | copy-start | bytes 196612
  27.5 0.6 %copy-start.10 = (bf16[256,128]{1,0:T(8,128)(2,1)}, bf16[256,128]{1,0:T(8,128)(2,1)S(1)}, u32[]{:S(2)}) copy-start(bf16[256,128]{1,0:T(8,128)(2,1)S(1)} %collective-permute-done.7.refs_5_) | copy-start | bytes 196612

commit v2 on v1

--- a/solution.py
+++ b/solution.py
@@ -76,8 +76,9 @@
     return (eye - 0.5 * block.astype(jnp.float32)).astype(jnp.bfloat16)
 
 
-def place_kernel(sizes, own_cols, other_cols, home, ypat, zpat, own, other, row, *messages):
+def place_kernel(sizes, own_cols, other_cols, home, ypat, zpat, own, other, flags, row, *messages):
     count, size = own.shape[1], own.shape[2]
+    n = len(LINKS)
     slots, valids = place(sizes)
     moved = home[0] != lax.axis_index("gz")
     cols = [jnp.where(moved, other_cols[0, k], own_cols[0, k]) for k in range(count)]
@@ -96,23 +97,28 @@
     row[0] = diag
     for q, message in enumerate(messages):
         slot, valid = slots[q], valids[q]
+        kept_y = (ypat[0, slot] == 1) & valid
+        kept_z = (zpat[0, slot] == 1) & valid
+        flags[q] = jnp.where(kept_y, 1, 0)
+        flags[n + q] = jnp.where(kept_z, 1, 0)
         block = pick(slot, valid)
         row[q + 1] = block
         message[0:size] = diag
-        message[size : 2 * size] = keep(ypat[0, slot] == 1, block)
-        flag = jnp.where(zpat[0, slot] == 1, 1.0, 0.0)
-        message[2 * size :] = jnp.full((message.shape[0] - 2 * size, size), flag, jnp.bfloat16)
+        message[size : 2 * size] = keep(kept_y, block)
+        message[2 * size :] = jnp.full(
+            (message.shape[0] - 2 * size, size), jnp.where(kept_z, 1.0, 0.0), jnp.bfloat16
+        )
 
 
 def unpack(message, size, valid):
     return message[0:size], keep(valid, message[size : 2 * size])
 
 
-def diagonal_kernel(sizes, ypat, zpat, row, *refs):
+def diagonal_kernel(sizes, flags, row, *refs):
     n = len(LINKS)
     messages, packed, ycol = refs[:n], refs[n], refs[n + 1]
     size = row.shape[1]
-    slots, valids = place(sizes)
+    _, valids = place(sizes)
     eye = eye_scaled(size)
     diag = row[0]
     t0 = corrected(eye, diag)
@@ -128,26 +134,25 @@
     y0 = total.astype(jnp.bfloat16)
     quad = mm(t0, y0)
     for q in range(n):
-        both = (ypat[0, slots[q]] == 1) & (zpat[0, slots[q]] == 1)
+        both = (flags[q] == 1) & (flags[n + q] == 1)
         quad += mm(half(keep(both, row[q + 1])), cols[q])
     packed[0:size] = y0
     packed[size:] = (eye - 0.5 * quad).astype(jnp.bfloat16)
 
 
-def between_kernel(sizes, ypat, row, packed, ycol, *refs):
+def between_kernel(sizes, flags, row, packed, ycol, *refs):
     n = len(LINKS)
     messages, yrow, yown = refs[:n], refs[n], refs[n + 1]
     size = row.shape[1]
-    slots, valids = place(sizes)
+    _, valids = place(sizes)
     eye = eye_scaled(size)
     diag, y0, tm0 = row[0], packed[0:size], packed[size:]
     total = mm(y0, tm0)
     for q in range(n):
         near_diag, facing = unpack(messages[q], size, valids[q])
         near_t = corrected(eye, near_diag)
-        kept = ypat[0, slots[q]] == 1
         block = row[q + 1]
-        y1 = keep(kept, (mm(diag, half(block)) + mm(block, near_t)).astype(jnp.bfloat16))
+        y1 = keep(flags[q] == 1, (mm(diag, half(block)) + mm(block, near_t)).astype(jnp.bfloat16))
         yrow[q] = y1
         zflag = messages[q][2 * size : 2 * size + 1, 0:1] > 0
         zfacing = jnp.where(zflag, half(facing), jnp.zeros_like(facing))
@@ -156,7 +161,7 @@
     yown[...] = total.astype(jnp.bfloat16)
 
 
-def last_kernel(sizes, ypat, zpat, row, packed, yrow, yown, *refs):
+def last_kernel(sizes, flags, row, packed, yrow, yown, *refs):
     n = len(LINKS)
     messages, arrived, zout, yout = refs[:n], refs[n : 2 * n], refs[2 * n], refs[2 * n + 1]
     size = row.shape[1]
@@ -167,21 +172,16 @@
     total = mm(tm0, t0)
     for q in range(n):
         slot = slots[q]
-        kept_y = ypat[0, slot] == 1
-        kept_z = zpat[0, slot] == 1
+        kept_y, kept_z = flags[q] == 1, flags[n + q] == 1
         near_diag, facing = unpack(messages[q], size, valids[q])
         near_t = corrected(eye, near_diag)
         near_y, near_tm = arrived[q][0:size], arrived[q][size:]
         zrow = half(keep(kept_y & kept_z, row[q + 1]))
         y1 = yrow[q]
         quad = mm(t0, y1) + mm(zrow, near_y)
-        tm = keep(kept_y & valids[q], (-0.5 * quad).astype(jnp.bfloat16))
-        yout[slot] = keep(
-            kept_y & valids[q], (mm(y0, tm) + mm(y1, near_tm)).astype(jnp.bfloat16)
-        )
-        zout[slot] = keep(
-            kept_z & valids[q], (mm(tm0, zrow) + mm(tm, near_t)).astype(jnp.bfloat16)
-        )
+        tm = keep(kept_y, (-0.5 * quad).astype(jnp.bfloat16))
+        yout[slot] = keep(kept_y, (mm(y0, tm) + mm(y1, near_tm)).astype(jnp.bfloat16))
+        zout[slot] = keep(kept_z, (mm(tm0, zrow) + mm(tm, near_t)).astype(jnp.bfloat16))
         zflag = messages[q][2 * size : 2 * size + 1, 0:1] > 0
         total += mm(tm, jnp.where(zflag, half(facing), jnp.zeros_like(facing)))
     absent = 11 - slots[-1]
@@ -191,14 +191,17 @@
     yout[0] = yown[...]
 
 
-def call(kernel, out_shapes, smem, vmem):
-    vspec = pl.BlockSpec(memory_space=pltpu.VMEM)
+def chip(*shape):
+    return pltpu.VMEM(shape, jnp.bfloat16)
+
+
+def call(kernel, outs, smem, vmem):
+    def spec(array):
+        return pl.BlockSpec(memory_space=pltpu.SMEM if array.dtype == jnp.int32 else pltpu.VMEM)
+
     return pl.pallas_call(
-        kernel,
-        out_shape=[jax.ShapeDtypeStruct(s, jnp.bfloat16) for s in out_shapes],
-        in_specs=[pl.BlockSpec(memory_space=pltpu.SMEM)] * len(smem) + [vspec] * len(vmem),
-        out_specs=[vspec] * len(out_shapes),
-    )(*smem, *vmem)
+        kernel, out_shape=outs, in_specs=[spec(a) for a in (*smem, *vmem)], out_specs=[spec(o) for o in outs]
+    )(*smem, *(pltpu.with_memory_space_constraint(v, pltpu.VMEM) for v in vmem))
 
 
 def body(sizes, s_blocks, s_columns, new_home, z_pattern, y_pattern):
@@ -211,30 +214,32 @@
 
     other = send(s_blocks, "z")
     other_cols = send(s_columns, "z")
-    row, *messages = call(
+    flags, row, *messages = call(
         functools.partial(place_kernel, sizes),
-        [(n + 1, size, size)] + [(2 * size + 16, size)] * n,
+        [pltpu.SMEM((2 * n,), jnp.int32), chip(n + 1, size, size)] + [chip(2 * size + 16, size)] * n,
         [s_columns, other_cols, new_home, y_pattern, z_pattern],
         [s_blocks, other],
     )
+    flags = pltpu.with_memory_space_constraint(flags, pltpu.SMEM)
     messages = [send(m, link) for m, link in zip(messages, LINKS)]
     packed, ycol = call(
         functools.partial(diagonal_kernel, sizes),
-        [(2 * size, size), (n, size, size)],
-        [y_pattern, z_pattern],
+        [chip(2 * size, size), chip(n, size, size)],
+        [flags],
         [row, *messages],
     )
     arrived = [send(packed, link) for link in LINKS]
     yrow, yown = call(
         functools.partial(between_kernel, sizes),
-        [(n, size, size), (size, size)],
-        [y_pattern],
+        [chip(n, size, size), chip(size, size)],
+        [flags],
         [row, packed, ycol, *messages],
     )
+    result = jax.ShapeDtypeStruct((PARTS, size, size), jnp.bfloat16)
     zout, yout = call(
         functools.partial(last_kernel, sizes),
-        [(PARTS, size, size)] * 2,
-        [y_pattern, z_pattern],
+        [result, result],
+        [flags],
         [row, packed, yrow, yown, *messages, *arrived],
     )
     return tuple(jnp.transpose(o, (1, 0, 2))[None] for o in (zout, yout))

time: 31.4 us -> 25.9 us (0.82)
  Pallas kernels: 9.96 us -> 4.03 us
  waiting for transfers between devices: 4.01 us -> 5.42 us
  local copies, waits for them, and re-layouts: 2.44 us -> 1.41 us
    pallas_call x4, Pallas kernels: 9.96 us -> 4.03 us  [call(): pl.pallas_call(kernel, out_shape=outs, in_specs=[spec(a) for a in (*smem,...]
    ppermute x12, waiting for transfers between devices: 4.01 us -> 5.42 us  [send(): return lax.ppermute(x, AXES, pairs[link])]
    unnamed x24 -> x4, local copies, waits for them, and re-layouts: 2.44 us -> 1.41 us
  transfers between devices with their start and end apart: 12 -> 12, of which waited for: 4 -> 4; matrix products, arithmetic and copies ran while one was open for 0% -> 0% of each run, Pallas kernels for 9% -> 3%
where the time goes in v2:
time: 25.9 us; the launch traced here: 25.8 us
  starting transfers between devices  13.6 us (53%)
  waiting for transfers between devices  5.42 us (21%)
  Pallas kernels  4.03 us (16%)
  local copies, waits for them, and re-layouts  1.41 us (5%)
  between operations  1.36 us (5%)
    ppermute x12, starting transfers between devices, send(): return lax.ppermute(x, AXES, pairs[link])  13.6 us
    ppermute x12, waiting for transfers between devices, send(): return lax.ppermute(x, AXES, pairs[link])  5.42 us
    pallas_call x4, Pallas kernels, call(): pl.pallas_call(kernel, out_shape=outs, in_specs=[spec(a) for a in (*smem,...  4.03 us
    unnamed x4, local copies, waits for them, and re-layouts  1.41 us
  transfers between devices with their start and end apart: 12, of which 4 were waited for; matrix products, arithmetic and copies ran while one was open for 0% of the time, Pallas kernels for 3%

profile of v2, /device:TPU:0, one launch (start us, length us, event | category | flops | bytes accessed | tf_op | source)
XLA Modules:
  0.0 25.8 jit_solution(12297752309749226705)
XLA Ops:
  0.6 0.6 %collective-permute-start.1 = (bf16[1,4,128,128]{3,2,1,0:T(8,128)(2,1)}, bf16[1,4,128,128]{3,2,1,0:T(8,128)(2,1)S(1)}, u32[]{:S(2)}, u32[]{:S(2)}) collective-permute-start(bf16[1,4,128,128]{3,2,1,0:T(8,128)(2,1)} %own.1), channel_id=1, source_target_pairs={{0,1},{1,0},{2,3},{3,2},{4,5},{5,4},{6,7},{7,6},{8,9},{9,8},{10,11... | collective-permute-start | bytes 393224 | tf_op jit(solution)/shard_map/ppermute | solution.py:213
  1.2 0.1 collective-permute-start
  1.9 0.6 %collective-permute-done.other_cols = s32[1,4]{1,0:T(1,128)S(1)} collective-permute-done((s32[1,4]{1,0:T(1,128)}, s32[1,4]{1,0:T(1,128)S(1)}, u32[]{:S(2)}, u32[]{:S(2)}) %collective-permute-start) | collective-permute-done | bytes 48 | tf_op jit(solution)/shard_map/ppermute | solution.py:213
  2.5 0.0 copy-start.1
  2.5 0.0 collective-permute-done.1.other
  2.5 0.5 %copy-done.1 = s32[1,4]{1,0:T(1,128)} copy-done((s32[1,4]{1,0:T(1,128)}, s32[1,4]{1,0:T(1,128)S(1)}, u32[]{:S(2)}) %copy-start.1) | copy-done | bytes 40
  3.0 0.0 copy-start
  3.0 0.9 %copy-done = bf16[1,4,128,128]{3,2,1,0:T(8,128)(2,1)S(1)} copy-done((bf16[1,4,128,128]{3,2,1,0:T(8,128)(2,1)S(1)}, bf16[1,4,128,128]{3,2,1,0:T(8,128)(2,1)}, u32[]{:S(2)}) %copy-start) | copy-done | bytes 131096
  3.9 0.8 %shard_map.68 = (s32[10]{0:T(128)S(4)}, bf16[6,128,128]{2,1,0:T(8,128)(2,1)S(1)}, bf16[272,128]{1,0:T(8,128)(2,1)S(1)}, bf16[272,128]{1,0:T(8,128)(2,1)S(1)}, bf...) custom-call(s32[1,4]{1,0:T(1,128)} %own_cols.1, s32[1,4]{1,0:T(1,128)} %copy-done.1, ...), custom_call_target="tpu_custom_call" | custom-call | tf_op jit(solution)/shard_map/pallas_call | solution.py:202
  4.8 2.8 %collective-permute-start.2 = (bf16[272,128]{1,0:T(8,128)(2,1)S(1)}, bf16[272,128]{1,0:T(8,128)(2,1)S(1)}, u32[]{:S(2)}, u32[]{:S(2)}) collective-permute-start(bf16[272,128]{1,0:T(8,128)(2,1)S(1)} %get-tuple-element.17), channel_id=1, source_target_pairs={{0,8},{1,9},{2,10},{3,11},{4,12},{5,13},{6,14},{7,15},{8,0},{9,1},... | collective-permute-start | bytes 208904 | tf_op jit(solution)/shard_map/ppermute | solution.py:213
  7.6 0.0 collective-permute-start.3
  7.6 1.6 %collective-permute-start.4 = (bf16[272,128]{1,0:T(8,128)(2,1)S(1)}, bf16[272,128]{1,0:T(8,128)(2,1)S(1)}, u32[]{:S(2)}, u32[]{:S(2)}) collective-permute-start(bf16[272,128]{1,0:T(8,128)(2,1)S(1)} %get-tuple-element.19), channel_id=1, source_target_pairs={{0,2},{1,3},{2,0},{3,1},{4,6},{5,7},{6,4},{7,5},{8,10},{9,11},{10,... | collective-permute-start | bytes 208904 | tf_op jit(solution)/shard_map/ppermute | solution.py:213
  9.1 0.2 collective-permute-start.5
  9.4 0.3 %collective-permute-start.6 = (bf16[272,128]{1,0:T(8,128)(2,1)S(1)}, bf16[272,128]{1,0:T(8,128)(2,1)S(1)}, u32[]{:S(2)}, u32[]{:S(2)}) collective-permute-start(bf16[272,128]{1,0:T(8,128)(2,1)S(1)} %get-tuple-element.21), channel_id=1, source_target_pairs={{0,1},{1,0},{2,3},{3,2},{4,5},{5,4},{6,7},{7,6},{8,9},{9,8},{10,11... | collective-permute-start | bytes 208904 | tf_op jit(solution)/shard_map/ppermute | solution.py:213
  9.6 0.5 %collective-permute-done.2.refs_0_ = bf16[272,128]{1,0:T(8,128)(2,1)S(1)} collective-permute-done((bf16[272,128]{1,0:T(8,128)(2,1)S(1)}, bf16[272,128]{1,0:T(8,128)(2,1)S(1)}, u32[]{:S(2)}, u32[]{:S(2)}) %collective-permute-start.2) | collective-permute-done | bytes 69664 | tf_op jit(solution)/shard_map/ppermute | solution.py:213
  10.1 0.0 collective-permute-done.3.refs_1_
  10.2 2.0 %collective-permute-done.4.refs_2_ = bf16[272,128]{1,0:T(8,128)(2,1)S(1)} collective-permute-done((bf16[272,128]{1,0:T(8,128)(2,1)S(1)}, bf16[272,128]{1,0:T(8,128)(2,1)S(1)}, u32[]{:S(2)}, u32[]{:S(2)}) %collective-permute-start.4) | collective-permute-done | bytes 69664 | tf_op jit(solution)/shard_map/ppermute | solution.py:213
  12.2 0.0 collective-permute-done.5.refs_3_
  12.2 0.0 collective-permute-done.6.refs_4_
  12.2 0.5 %shard_map.69 = (bf16[256,128]{1,0:T(8,128)(2,1)S(1)}, bf16[5,128,128]{2,1,0:T(8,128)(2,1)S(1)}) custom-call(s32[10]{0:T(128)S(4)} %get-tuple-element.15.flags, bf16[6,128,128]{2,1,0:T(8,128)(2,1)S(1)} %get-tuple-element.16.row, bf16[272,128]{1,0:T(8,128)(2,1)S(1)} %collective-permute-done.2.refs_0_, bf16[272,128]{1,0:T(8,128)(2,1)S(1)} %collective-permute-done.3.refs_1_, ...), custom_call_target="tpu_custom_call" | custom-call | tf_op jit(solution)/shard_map/pallas_call | solution.py:202
  12.7 0.1 collective-permute-start.11
  12.7 0.5 %collective-permute-start.10 = (bf16[256,128]{1,0:T(8,128)(2,1)S(1)}, bf16[256,128]{1,0:T(8,128)(2,1)S(1)}, u32[]{:S(2)}, u32[]{:S(2)}) collective-permute-start(bf16[256,128]{1,0:T(8,128)(2,1)S(1)} %get-tuple-element.22.packed), channel_id=1, source_target_pairs={{0,1},{1,0},{2,4},{3,5},{4,2},{5,3},{6,7},{7,6},{8,9},{9,8},{10,12... | collective-permute-start | bytes 196616 | tf_op jit(solution)/shard_map/ppermute | solution.py:213
  13.2 4.0 %collective-permute-start.9 = (bf16[256,128]{1,0:T(8,128)(2,1)S(1)}, bf16[256,128]{1,0:T(8,128)(2,1)S(1)}, u32[]{:S(2)}, u32[]{:S(2)}) collective-permute-start(bf16[256,128]{1,0:T(8,128)(2,1)S(1)} %get-tuple-element.22.packed), channel_id=1, source_target_pairs={{0,2},{1,3},{2,0},{3,1},{4,6},{5,7},{6,4},{7,5},{8,10},{9,11},{10,... | collective-permute-start | bytes 196616 | tf_op jit(solution)/shard_map/ppermute | solution.py:213
  17.3 0.0 collective-permute-start.8
  17.3 3.4 %collective-permute-start.7 = (bf16[256,128]{1,0:T(8,128)(2,1)S(1)}, bf16[256,128]{1,0:T(8,128)(2,1)S(1)}, u32[]{:S(2)}, u32[]{:S(2)}) collective-permute-start(bf16[256,128]{1,0:T(8,128)(2,1)S(1)} %get-tuple-element.22.packed), channel_id=1, source_target_pairs={{0,8},{1,9},{2,10},{3,11},{4,12},{5,13},{6,14},{7,15},{8,0},{9,1},... | collective-permute-start | bytes 196616 | tf_op jit(solution)/shard_map/ppermute | solution.py:213
  20.7 0.9 %shard_map.70 = (bf16[5,128,128]{2,1,0:T(8,128)(2,1)S(1)}, bf16[128,128]{1,0:T(8,128)(2,1)S(1)}) custom-call(s32[10]{0:T(128)S(4)} %get-tuple-element.15.flags, bf16[6,128,128]{2,1,0:T(8,128)(2,1)S(1)} %get-tuple-element.16.row, bf16[256,128]{1,0:T(8,128)(2,1)S(1)} %get-tuple-element.22.packed, bf16[5,128,128]{2,1,0:T(8,128)(2,1)S(1)} %get-tuple-element.23.ycol, ...), custom_call_target="tpu_custom_call" | custom-call | tf_op jit(solution)/shard_map/pallas_call | solution.py:202
  21.6 0.0 collective-permute-done.11.refs_9_
  21.6 0.0 collective-permute-done.10.refs_8_
  21.6 0.0 collective-permute-done.9.refs_7_
  21.6 0.0 collective-permute-done.8.refs_6_
  21.6 2.3 %collective-permute-done.7.refs_5_ = bf16[256,128]{1,0:T(8,128)(2,1)S(1)} collective-permute-done((bf16[256,128]{1,0:T(8,128)(2,1)S(1)}, bf16[256,128]{1,0:T(8,128)(2,1)S(1)}, u32[]{:S(2)}, u32[]{:S(2)}) %collective-permute-start.7) | collective-permute-done | bytes 65568 | tf_op jit(solution)/shard_map/ppermute | solution.py:213
  24.0 1.8 %shard_map.71 = (bf16[7,128,128]{2,1,0:T(8,128)(2,1)}, bf16[7,128,128]{2,1,0:T(8,128)(2,1)}) custom-call(s32[10]{0:T(128)S(4)} %get-tuple-element.15.flags, bf16[6,128,128]{2,1,0:T(8,128)(2,1)S(1)} %get-tuple-element.16.row, bf16[256,128]{1,0:T(8,128)(2,1)S(1)} %get-tuple-element.22.packed, bf16[5,128,128]{2,1,0:T(8,128)(2,1)S(1)} %get-tuple-element.24.yrow, ...), custom_call_target="tpu_custom_call" | custom-call | tf_op jit(solution)/shard_map/pallas_call | solution.py:202
Async XLA Ops:
  0.6 1.9 %collective-permute-start.1 = (bf16[1,4,128,128]{3,2,1,0:T(8,128)(2,1)}, bf16[1,4,128,128]{3,2,1,0:T(8,128)(2,1)S(1)}, u32[]{:S(2)}, u32[]{:S(2)}) collective-permute-start(bf16[1,4,128,128]{3,2,1,0:T(8,128)(2,1)} %own.1), channel_id=1, source_target_pairs={{0,1},{1,0},{2,3},{3,2},{4,5},{5,4},{6,7},{7,6},{8,9},{9,8},{10,11... | collective-permute-start | bytes 393224 | tf_op jit(solution)/shard_map/ppermute | solution.py:213
  1.2 1.3 %collective-permute-start = (s32[1,4]{1,0:T(1,128)}, s32[1,4]{1,0:T(1,128)S(1)}, u32[]{:S(2)}, u32[]{:S(2)}) collective-permute-start(s32[1,4]{1,0:T(1,128)} %own_cols.1), channel_id=1, source_target_pairs={{0,1},{1,0},{2,3},{3,2},{4,5},{5,4},{6,7},{7,6},{8,9},{9,8},{10,11... | collective-permute-start | bytes 56 | tf_op jit(solution)/shard_map/ppermute | solution.py:213
  2.5 0.5 %copy-start.1 = (s32[1,4]{1,0:T(1,128)}, s32[1,4]{1,0:T(1,128)S(1)}, u32[]{:S(2)}) copy-start(s32[1,4]{1,0:T(1,128)S(1)} %collective-permute-done.other_cols) | copy-start | bytes 52
  3.0 0.9 %copy-start = (bf16[1,4,128,128]{3,2,1,0:T(8,128)(2,1)S(1)}, bf16[1,4,128,128]{3,2,1,0:T(8,128)(2,1)}, u32[]{:S(2)}) copy-start(bf16[1,4,128,128]{3,2,1,0:T(8,128)(2,1)} %own.1) | copy-start | bytes 393220
  4.8 5.4 %collective-permute-start.2 = (bf16[272,128]{1,0:T(8,128)(2,1)S(1)}, bf16[272,128]{1,0:T(8,128)(2,1)S(1)}, u32[]{:S(2)}, u32[]{:S(2)}) collective-permute-start(bf16[272,128]{1,0:T(8,128)(2,1)S(1)} %get-tuple-element.17), channel_id=1, source_target_pairs={{0,8},{1,9},{2,10},{3,11},{4,12},{5,13},{6,14},{7,15},{8,0},{9,1},... | collective-permute-start | bytes 208904 | tf_op jit(solution)/shard_map/ppermute | solution.py:213
  7.6 2.6 %collective-permute-start.3 = (bf16[272,128]{1,0:T(8,128)(2,1)S(1)}, bf16[272,128]{1,0:T(8,128)(2,1)S(1)}, u32[]{:S(2)}, u32[]{:S(2)}) collective-permute-start(bf16[272,128]{1,0:T(8,128)(2,1)S(1)} %get-tuple-element.18), channel_id=1, source_target_pairs={{0,1},{1,0},{2,3},{3,2},{4,5},{5,4},{6,7},{7,6},{8,16},{9,17},{10,... | collective-permute-start | bytes 208904 | tf_op jit(solution)/shard_map/ppermute | solution.py:213
  7.6 4.6 %collective-permute-start.4 = (bf16[272,128]{1,0:T(8,128)(2,1)S(1)}, bf16[272,128]{1,0:T(8,128)(2,1)S(1)}, u32[]{:S(2)}, u32[]{:S(2)}) collective-permute-start(bf16[272,128]{1,0:T(8,128)(2,1)S(1)} %get-tuple-element.19), channel_id=1, source_target_pairs={{0,2},{1,3},{2,0},{3,1},{4,6},{5,7},{6,4},{7,5},{8,10},{9,11},{10,... | collective-permute-start | bytes 208904 | tf_op jit(solution)/shard_map/ppermute | solution.py:213
  9.1 3.0 %collective-permute-start.5 = (bf16[272,128]{1,0:T(8,128)(2,1)S(1)}, bf16[272,128]{1,0:T(8,128)(2,1)S(1)}, u32[]{:S(2)}, u32[]{:S(2)}) collective-permute-start(bf16[272,128]{1,0:T(8,128)(2,1)S(1)} %get-tuple-element.20), channel_id=1, source_target_pairs={{0,1},{1,0},{2,4},{3,5},{4,2},{5,3},{6,7},{7,6},{8,9},{9,8},{10,12... | collective-permute-start | bytes 208904 | tf_op jit(solution)/shard_map/ppermute | solution.py:213
  9.4 2.8 %collective-permute-start.6 = (bf16[272,128]{1,0:T(8,128)(2,1)S(1)}, bf16[272,128]{1,0:T(8,128)(2,1)S(1)}, u32[]{:S(2)}, u32[]{:S(2)}) collective-permute-start(bf16[272,128]{1,0:T(8,128)(2,1)S(1)} %get-tuple-element.21), channel_id=1, source_target_pairs={{0,1},{1,0},{2,3},{3,2},{4,5},{5,4},{6,7},{7,6},{8,9},{9,8},{10,11... | collective-permute-start | bytes 208904 | tf_op jit(solution)/shard_map/ppermute | solution.py:213
  12.7 8.9 %collective-permute-start.11 = (bf16[256,128]{1,0:T(8,128)(2,1)S(1)}, bf16[256,128]{1,0:T(8,128)(2,1)S(1)}, u32[]{:S(2)}, u32[]{:S(2)}) collective-permute-start(bf16[256,128]{1,0:T(8,128)(2,1)S(1)} %get-tuple-element.22.packed), channel_id=1, source_target_pairs={{0,1},{1,0},{2,3},{3,2},{4,5},{5,4},{6,7},{7,6},{8,9},{9,8},{10,11... | collective-permute-start | bytes 196616 | tf_op jit(solution)/shard_map/ppermute | solution.py:213
  12.7 8.9 %collective-permute-start.10 = (bf16[256,128]{1,0:T(8,128)(2,1)S(1)}, bf16[256,128]{1,0:T(8,128)(2,1)S(1)}, u32[]{:S(2)}, u32[]{:S(2)}) collective-permute-start(bf16[256,128]{1,0:T(8,128)(2,1)S(1)} %get-tuple-element.22.packed), channel_id=1, source_target_pairs={{0,1},{1,0},{2,4},{3,5},{4,2},{5,3},{6,7},{7,6},{8,9},{9,8},{10,12... | collective-permute-start | bytes 196616 | tf_op jit(solution)/shard_map/ppermute | solution.py:213
  13.2 8.4 %collective-permute-start.9 = (bf16[256,128]{1,0:T(8,128)(2,1)S(1)}, bf16[256,128]{1,0:T(8,128)(2,1)S(1)}, u32[]{:S(2)}, u32[]{:S(2)}) collective-permute-start(bf16[256,128]{1,0:T(8,128)(2,1)S(1)} %get-tuple-element.22.packed), channel_id=1, source_target_pairs={{0,2},{1,3},{2,0},{3,1},{4,6},{5,7},{6,4},{7,5},{8,10},{9,11},{10,... | collective-permute-start | bytes 196616 | tf_op jit(solution)/shard_map/ppermute | solution.py:213
  17.3 4.4 %collective-permute-start.8 = (bf16[256,128]{1,0:T(8,128)(2,1)S(1)}, bf16[256,128]{1,0:T(8,128)(2,1)S(1)}, u32[]{:S(2)}, u32[]{:S(2)}) collective-permute-start(bf16[256,128]{1,0:T(8,128)(2,1)S(1)} %get-tuple-element.22.packed), channel_id=1, source_target_pairs={{0,1},{1,0},{2,3},{3,2},{4,5},{5,4},{6,7},{7,6},{8,16},{9,17},{10,... | collective-permute-start | bytes 196616 | tf_op jit(solution)/shard_map/ppermute | solution.py:213
  17.3 6.7 %collective-permute-start.7 = (bf16[256,128]{1,0:T(8,128)(2,1)S(1)}, bf16[256,128]{1,0:T(8,128)(2,1)S(1)}, u32[]{:S(2)}, u32[]{:S(2)}) collective-permute-start(bf16[256,128]{1,0:T(8,128)(2,1)S(1)} %get-tuple-element.22.packed), channel_id=1, source_target_pairs={{0,8},{1,9},{2,10},{3,11},{4,12},{5,13},{6,14},{7,15},{8,0},{9,1},... | collective-permute-start | bytes 196616 | tf_op jit(solution)/shard_map/ppermute | solution.py:213
